TPU v7x, 32 devices: a whole 2x2x4 slice. The times are simulated.
32 devices in a mesh: grp: 8 (over z, x), slc: 4 (over y, core).
Axes of the slice: x: 2, y: 2, z: 4, core: 2. Of those that a mesh axis runs over, the one named last changes fastest.
Arguments:
- orbitals: float32 [64, 48, 2304], P('grp', 'slc'), may hold values from -6 to 6
- local_pot: float32 [64, 48, 2304], P('grp', 'slc'), may hold values from -1 to 1
- pair_owner: int32 [8, 8, 1], P('grp'), may hold values from 0 to 7; in each aligned block of 8 rows (0 to 7, 8 to 15, ..., all dimensions but the last counted through in order) at most 2 rows name the same one
- pair_remote: int32 [8, 8], P('grp'), may hold values from 0 to 7
- pair_resident: int32 [8, 8], P('grp'), may hold values from 0 to 1
- pair_count: int32 [8, 4], P('grp'), may hold values from 1 to 3, 8 in all within a row
- offsets: int32 [64, 3], replicated, may hold values from 0 to 23
Outputs:
- applied: float32 [64, 48, 2304], P('grp', 'slc')
Inputs may be any that keep to these rules, and one draw needn't show every extreme that they name: `pair_owner`: within one group's 8 pairs no owner group is named more than 2 times, and some owner group is named exactly 2 times. `pair_count`: the 4 counts of one group sum to 8, and in every group some device has exactly 3.
All inputs are finite; a program needn't handle non-finite values.
Results may differ from a plain program's by a relative error of at most 0.0003.
Values sent between devices are 32-bit elements; how exact they have to be, the bound alone decides.
No kernel may reach another device: no remote copies, remote signals or barrier semaphores. Data moves between devices by JAX's collectives and lax.ppermute only.
A program may use at most 128 MiB of HBM per device.

v0:
```python
import functools
import jax
import jax.numpy as jnp
import numpy as np
from jax import lax
from jax.experimental import pallas as pl
from jax.experimental.pallas import tpu as pltpu
from jax.sharding import PartitionSpec as P


B = 48
CAP = 2
LANES = 128
COLS = B * B // LANES
BLK = 3 * LANES
ROWS_BLK = BLK // B
NBLK = COLS // 3
PITCH = 56
PAD = (B // 2) * COLS
BOX = B * COLS


def sine_np():
    k = np.arange(B)
    return (np.sqrt(2.0 / (B + 1)) * np.sin(np.pi * (k[:, None] + 1) * (k[None, :] + 1) / (B + 1.0))).astype(
        np.float32
    )


def lam_np():
    k = np.arange(B)
    return 2.0 - 2.0 * np.cos(np.pi * (k + 1.0) / (B + 1.0))


def split(x):
    high = x.astype(jnp.bfloat16)
    return high, (x - high.astype(jnp.float32)).astype(jnp.bfloat16)


def mm(a, b):
    return jnp.dot(a, b, preferred_element_type=jnp.float32)


def mm3(ah, al, bh, bl):
    return mm(ah, bh) + mm(al, bh) + mm(ah, bl)


FWD_K = ((0, 128), (0, 256), (128, 384), (256, 384))


def tables_kernel(sine, wide, lams, after, sine3, fwd_h, fwd_l, inv_h, inv_l, weight):
    q = sine[...]
    qh, ql = split(q)
    q48h, q48l = qh[:, :B], ql[:, :B]
    sine3[...] = jnp.concatenate([q48h, q48h, q48l], axis=1)
    fwd_h[...] = jnp.zeros(fwd_h.shape, jnp.bfloat16)
    fwd_l[...] = jnp.zeros(fwd_l.shape, jnp.bfloat16)
    for b in range(ROWS_BLK):
        fwd_h[b * B : (b + 1) * B, b * LANES : (b + 1) * LANES] = qh
        fwd_l[b * B : (b + 1) * B, b * LANES : (b + 1) * LANES] = ql
    lane = lax.broadcasted_iota(jnp.int32, (LANES, BLK), 1)
    w = jnp.concatenate([wide[...], jnp.zeros((LANES - B, BLK), jnp.float32)], axis=0)
    for b in range(ROWS_BLK):
        part = jnp.where((lane >= b * B) & (lane < (b + 1) * B), w, 0.0)
        ph, plo = split(part)
        inv_h[b * LANES : (b + 1) * LANES, :] = ph
        inv_l[b * LANES : (b + 1) * LANES, :] = plo
    pair = lams[...]
    for k, lam in enumerate(lam_np()):
        weight[:, k * LANES : (k + 1) * LANES] = 1.0 / (pair + np.float32(lam))


def make_tables(after):
    q = sine_np()
    padded = np.zeros((B, LANES), np.float32)
    padded[:, :B] = q
    wide = np.tile(q, (1, ROWS_BLK))
    lam = lam_np()
    lam3 = np.ones((LANES,))
    lam3[:B] = lam
    lams = (lam[:, None] + lam3[None, :]).astype(np.float32)
    wide_shape, tall_shape = (BLK, ROWS_BLK * LANES), (ROWS_BLK * LANES, BLK)
    shapes = (
        pltpu.VMEM((B, 3 * B), jnp.bfloat16),
        pltpu.VMEM(wide_shape, jnp.bfloat16),
        pltpu.VMEM(wide_shape, jnp.bfloat16),
        pltpu.VMEM(tall_shape, jnp.bfloat16),
        pltpu.VMEM(tall_shape, jnp.bfloat16),
        pltpu.VMEM((B, B * LANES), jnp.float32),
    )
    return pl.pallas_call(
        tables_kernel,
        in_specs=[vmem()] * 3 + [smem()],
        out_specs=[vmem()] * len(shapes),
        out_shape=shapes,
        compiler_params=grant(8),
        name="tables",
    )(jnp.asarray(padded), jnp.asarray(wide), jnp.asarray(lams), after)


def one_slot(near, box, shifted, left_h, left_l, mid, mid2, inv_lh, inv_ll, sine3, fwd_h, fwd_l, inv_h, inv_l, weight, spots, out, e0, e1, e2):
    lane = lax.broadcasted_iota(jnp.int32, (B, LANES), 1)

    def turned(source, d0, d1, d2, j_list):
        flat = d0 * (B * B) + d1 * B + d2
        rows = lax.shift_right_arithmetic(flat, 7)
        rest = flat & (LANES - 1)
        back = (LANES - rest) & (LANES - 1)
        rolled = {}
        for j in j_list + [j_list[-1] + 1]:
            rolled[j] = pltpu.roll(source[pl.ds(PAD + rows + j, B, stride=COLS), :], back, axis=1)
        results = []
        for j in j_list:
            moved = jnp.where(lane < LANES - rest, rolled[j], rolled[j + 1])
            bb = spots[j : j + 1, :] + d1
            cc = spots[COLS + j : COLS + j + 1, :] + d2
            inside = (bb >= 0) & (bb < B) & (cc >= 0) & (cc < B)
            results.append(jnp.where(inside, moved, 0.0))
        return results

    s3 = sine3[...]

    def along_first(x):
        xh, xl = split(x)
        return mm(s3, jnp.concatenate([xh, xl, xh], axis=0))

    for m in range(NBLK):
        js = [3 * m, 3 * m + 1, 3 * m + 2]
        parts = turned(box, e0, e1, e2, js)
        dens = []
        for j, part in zip(js, parts):
            shifted[j * B : (j + 1) * B, :] = part
            dens.append(part * near[pl.ds(j, B, stride=COLS), :])
        yh, yl = split(along_first(jnp.concatenate(dens, axis=1)))
        left_h[m * B : (m + 1) * B, :] = yh
        left_l[m * B : (m + 1) * B, :] = yl
    for p, (lo, hi) in enumerate(FWD_K):
        cols = slice(p * 2 * LANES, (p + 1) * 2 * LANES)
        y = mm3(left_h[:, lo:hi], left_l[:, lo:hi], fwd_h[lo:hi, cols], fwd_l[lo:hi, cols])
        for m in range(NBLK):
            for h in range(2):
                b = ROWS_BLK * m + 2 * p + h
                mid[pl.ds(b, B, stride=PITCH), :] = y[m * B : (m + 1) * B, h * LANES : (h + 1) * LANES]
    group = 6

    def second(i, carry):
        first = i * group
        z = jnp.concatenate(
            [mid[pl.ds(pl.multiple_of((first + u) * PITCH, 8), B), :] for u in range(group)], axis=1
        )
        y = along_first(z) * weight[:, pl.ds(pl.multiple_of(first * LANES, LANES), group * LANES)]
        y = along_first(y)
        for u in range(group):
            mid2[pl.ds(first + u, B, stride=PITCH), :] = y[:, u * LANES : (u + 1) * LANES]
        return carry

    lax.fori_loop(0, B // group, second, 0)
    for m in range(NBLK):
        for b in range(ROWS_BLK):
            start = (ROWS_BLK * m + b) * PITCH
            zh, zl = split(mid2[start : start + B, :])
            inv_lh[m * B : (m + 1) * B, b * LANES : (b + 1) * LANES] = zh
            inv_ll[m * B : (m + 1) * B, b * LANES : (b + 1) * LANES] = zl
    ka = slice(0, 6 * LANES)
    kb = slice(5 * LANES, 8 * LANES)
    ya = mm3(inv_lh[:, ka], inv_ll[:, ka], inv_h[ka, : 2 * LANES], inv_l[ka, : 2 * LANES])
    yb = mm3(inv_lh[:, kb], inv_ll[:, kb], inv_h[kb, 2 * LANES :], inv_l[kb, 2 * LANES :])
    for m in range(NBLK):
        y = jnp.concatenate([ya[m * B : (m + 1) * B], yb[m * B : (m + 1) * B]], axis=1)
        pot = along_first(y)
        for u in range(3):
            j = 3 * m + u
            part = pot[:, u * LANES : (u + 1) * LANES]
            box[pl.ds(PAD + j, B, stride=COLS), :] = part * near[pl.ds(j, B, stride=COLS), :]
            out[0, pl.ds(j, B, stride=COLS), :] = part * shifted[j * B : (j + 1) * B, :]
    for m in range(NBLK):
        js = [3 * m, 3 * m + 1, 3 * m + 2]
        for j, part in zip(js, turned(box, -e0, -e1, -e2, js)):
            out[1, pl.ds(j, B, stride=COLS), :] = part


def pair_kernel(slices, slab, round_id, meta, tab, after, *refs):
    nears, refs = refs[:slices], refs[slices:]
    fars, refs = refs[:slices], refs[slices:]
    consts, refs = refs[:7], refs[7:]
    near_outs, refs = refs[:slices], refs[slices:]
    far_outs, refs = refs[:slices], refs[slices:]
    token, refs = refs[0], refs[1:]
    token[0] = after[0]
    near, box, shifted, left_h, left_l, mid, mid2, inv_lh, inv_ll, out = refs
    own = meta[1]
    zeros = jnp.zeros((PAD, LANES), jnp.float32)
    box[:PAD, :] = zeros
    box[PAD + BOX :, :] = zeros
    for c in range(CAP):
        slot = (round_id * slices + own) * CAP + c

        @pl.when(tab[0, slot] > 0)
        def _():
            for k in range(slices):
                start = (own ^ k) * slab
                near[pl.ds(start, slab), :] = nears[k][round_id * CAP + c]
                box[pl.ds(PAD + start, slab), :] = fars[k][c]
            one_slot(near, box, shifted, left_h, left_l, mid, mid2, inv_lh, inv_ll, *consts, out, tab[2, slot], tab[3, slot], tab[4, slot])
            for k in range(slices):
                start = (own ^ k) * slab
                near_outs[k][c] = out[0, pl.ds(start, slab), :]
                far_outs[k][c] = out[1, pl.ds(start, slab), :]


def kept(x):
    return pltpu.with_memory_space_constraint(x, pltpu.VMEM)


def grant(mib):
    return pltpu.CompilerParams(vmem_limit_bytes=mib * 2**20)


def smem():
    return pl.BlockSpec(memory_space=pltpu.SMEM)


def vmem():
    return pl.BlockSpec(memory_space=pltpu.VMEM)


def pair_call(slices, slab, round_id, meta, tab, after, nears, fars, consts):
    spots = np.arange(B * B).reshape(COLS, LANES)
    spots = jnp.asarray(np.concatenate([spots // B, spots % B]).astype(np.int32))
    outs = pl.pallas_call(
        functools.partial(pair_kernel, slices, slab, round_id),
        in_specs=[smem()] * 3 + [vmem()] * (2 * slices + 7),
        out_specs=[vmem()] * (2 * slices) + [smem()],
        out_shape=[pltpu.VMEM((CAP, slab, LANES), jnp.float32)] * (2 * slices) + [jax.ShapeDtypeStruct((1,), jnp.int32)],
        scratch_shapes=[
            pltpu.VMEM((BOX, LANES), jnp.float32),
            pltpu.VMEM((BOX + 2 * PAD, LANES), jnp.float32),
            pltpu.VMEM((BOX, LANES), jnp.float32),
            pltpu.VMEM((NBLK * B, BLK), jnp.bfloat16),
            pltpu.VMEM((NBLK * B, BLK), jnp.bfloat16),
            pltpu.VMEM((B * PITCH, LANES), jnp.float32),
            pltpu.VMEM((B * PITCH, LANES), jnp.float32),
            pltpu.VMEM((NBLK * B, ROWS_BLK * LANES), jnp.bfloat16),
            pltpu.VMEM((NBLK * B, ROWS_BLK * LANES), jnp.bfloat16),
            pltpu.VMEM((2, BOX, LANES), jnp.float32),
        ],
        cost_estimate=pl.CostEstimate(flops=2 * 10**9, transcendentals=0, bytes_accessed=8 * 10**6),
        compiler_params=grant(24),
    )(meta, tab, after, *map(kept, nears), *map(kept, fars), *map(kept, consts), spots)
    return outs[:slices], outs[slices : 2 * slices], outs[-1]


def slab_pieces(orbs, planes, o):
    if orbs == 8:
        return [(o, planes * COLS, 0)]
    tiles = orbs // 8
    high = lax.shift_right_logical(o, 3)
    return [((a * tiles + high) * COLS * 8 + (o & 7), COLS, a * COLS) for a in range(planes)]


def near_kernel(groups, slices, listed, orbs, planes, meta, values, *refs):
    outs, (tab, seen) = refs[:slices], refs[slices:]
    gid = meta[0]
    own = meta[1]
    owner_at, remote_at, resident_at, count_at = 2, 2 + listed, 2 + 2 * listed, 2 + 3 * listed
    offset_at = count_at + slices
    for g in range(groups):
        seen[g] = 0
    for n in range(groups * CAP):
        tab[0, n] = 0

    def place(t, carry):
        running = 0
        home = 0
        for u in range(slices):
            running = running + meta[count_at + u]
            home = home + jnp.where(running <= t, 1, 0)
        owner = meta[owner_at + t]
        rank = seen[owner]
        seen[owner] = rank + 1
        n = (gid ^ owner) * CAP + rank
        local = home * (orbs // slices) + meta[resident_at + t]
        near_at = offset_at + 3 * (gid * orbs + local)
        far_at = offset_at + 3 * (owner * orbs + meta[remote_at + t])
        tab[0, n] = 1
        tab[1, n] = local
        for d in range(3):
            tab[2 + d, n] = meta[near_at + d] - meta[far_at + d]
        return carry

    lax.fori_loop(0, listed, place, 0)
    for k in range(slices):
        for q in range(groups // slices):
            for c in range(CAP):
                n = (q * slices + (own ^ k)) * CAP + c

                @pl.when(tab[0, n] > 0)
                def _():
                    for start, count, to in slab_pieces(orbs, planes, tab[1, n]):
                        outs[k][q * CAP + c, to : to + count, :] = values[pl.ds(start, count, stride=8), :]


def far_kernel(groups, slices, listed, orbs, planes, lists, values, *refs):
    rounds = groups // slices
    outs, (tab, after) = refs[: rounds * slices], refs[rounds * slices :]
    gid = lists[0, 2 * listed]
    own = lists[0, 2 * listed + 1]
    after[0] = own
    for n in range(groups * CAP):
        tab[0, n] = 0

    def place(r, carry):
        def look(t, rank):
            hit = lists[gid ^ r, t] == gid

            @pl.when(hit)
            def _():
                tab[0, r * CAP + rank] = 1
                tab[1, r * CAP + rank] = lists[gid ^ r, listed + t]

            return rank + jnp.where(hit, 1, 0)

        return lax.fori_loop(0, listed, look, carry * 0)

    lax.fori_loop(0, groups, place, 0)
    for q in range(rounds):
        for k in range(slices):
            for c in range(CAP):
                n = (q * slices + (own ^ k)) * CAP + c

                @pl.when(tab[0, n] > 0)
                def _():
                    for start, count, to in slab_pieces(orbs, planes, tab[1, n]):
                        outs[q * slices + k][c, to : to + count, :] = values[pl.ds(start, count, stride=8), :]


def sum_kernel(slices, orbs, planes, rounds, first, meta, near_tab, far_tab, base, *refs):
    if first:
        values, refs = refs[0], refs[1:]
    count = len(rounds) * slices
    nears, fars, out = refs[:count], refs[count : 2 * count], refs[-1]
    own = meta[1]
    out[...] = base[...] * values[...] if first else base[...]
    for tab, parts in ((near_tab, nears), (far_tab, fars)):
        for at, q in enumerate(rounds):
            for k in range(slices):
                for c in range(CAP):
                    n = (q * slices + (own ^ k)) * CAP + c

                    @pl.when(tab[0, n] > 0)
                    def _():
                        for start, count, to in slab_pieces(orbs, planes, tab[1, n]):
                            rows = pl.ds(start, count, stride=8)
                            out[rows, :] = out[rows, :] - parts[at * slices + k][c, to : to + count, :]


def as_rows(x):
    orbs, planes, cells = x.shape
    x = x.transpose(1, 0, 2).reshape(planes, orbs // 8, 8, cells // LANES, LANES)
    return x.transpose(0, 1, 3, 2, 4).reshape(-1, LANES)


def operator(orbitals, local_pot, pair_owner, pair_remote, pair_resident, pair_count, offsets):
    groups = lax.axis_size("grp")
    slices = lax.axis_size("slc")
    orbs, planes, cells = orbitals.shape
    listed = pair_owner.shape[1]
    rounds = groups // slices
    slab = planes * cells // LANES
    gid = lax.axis_index("grp").astype(jnp.int32)
    sid = lax.axis_index("slc").astype(jnp.int32)
    owner = pair_owner[0, :, 0]
    meta = jnp.concatenate(
        [gid[None], sid[None], owner, pair_remote[0], pair_resident[0], pair_count[0], offsets.reshape(-1)]
    )
    where = lax.broadcasted_iota(jnp.int32, (groups, 2), 0)
    where = jnp.where(lax.broadcasted_iota(jnp.int32, (groups, 2), 1) == 0, where, sid)
    mine = jnp.concatenate([owner, pair_remote[0]])
    mine = jnp.concatenate([jnp.broadcast_to(mine[None], (groups, 2 * listed)), where], axis=1)
    lists = lax.all_to_all(mine, "grp", 0, 0, tiled=True)
    rows = as_rows(orbitals)
    pot_rows = as_rows(local_pot)
    sizes = (groups, slices, listed, orbs, planes)
    keys = [(q, k) for q in range(rounds) for k in range(slices)]
    word = jax.ShapeDtypeStruct((1,), jnp.int32)
    packed = pl.pallas_call(
        functools.partial(near_kernel, *sizes),
        in_specs=[smem(), vmem()],
        out_specs=[vmem()] * slices + [smem()],
        out_shape=[pltpu.VMEM((rounds * CAP, slab, LANES), jnp.float32)] * slices
        + [jax.ShapeDtypeStruct((5, groups * CAP), jnp.int32)],
        scratch_shapes=[pltpu.SMEM((groups,), jnp.int32)],
        compiler_params=grant(4),
        name="near_pack",
    )(meta, rows)
    near_tab = packed[slices]
    across = [[(s, s ^ k) for s in range(slices)] for k in range(slices)]
    nears = [packed[0]]
    for k in range(1, slices):
        nears.append(lax.ppermute(packed[k], "slc", across[k]))
    sends = pl.pallas_call(
        functools.partial(far_kernel, *sizes),
        in_specs=[smem(), vmem()],
        out_specs=[vmem()] * len(keys) + [smem()] * 2,
        out_shape=[pltpu.VMEM((CAP, slab, LANES), jnp.float32)] * len(keys)
        + [jax.ShapeDtypeStruct((2, groups * CAP), jnp.int32), word],
        compiler_params=grant(4),
        name="far_pack",
    )(lists, rows)
    far_tab, after = sends[-2], sends[-1]

    def there(q, k):
        return [
            (g * slices + s, (g ^ (q * slices + (s ^ k))) * slices + (s ^ k))
            for g in range(groups)
            for s in range(slices)
        ]

    fars = {}
    for q, k in keys:
        fars[q, k] = lax.ppermute(sends[q * slices + k], ("grp", "slc"), there(q, k))
    consts = make_tables(after)
    near_back, far_back = {}, {}
    for q in range(rounds):
        near_out, far_out, after = pair_call(
            slices, slab, q, meta, near_tab, after, nears, [fars[q, k] for k in range(slices)], consts
        )
        for k in range(slices):
            back = [(d, s) for s, d in there(q, k)]
            far_back[q, k] = lax.ppermute(far_out[k], ("grp", "slc"), back)
            near_back[q, k] = near_out[k] if k == 0 else lax.ppermute(near_out[k], "slc", across[k])
    out = None
    for chosen in (tuple(range(rounds - 1)), (rounds - 1,)):
        first = out is None
        base = [pot_rows, rows] if first else [out]
        part = [x for x in keys if x[0] in chosen]
        parts = [kept(near_back[x]) for x in part] + [kept(far_back[x]) for x in part]
        out = pl.pallas_call(
            functools.partial(sum_kernel, slices, orbs, planes, chosen, first),
            in_specs=[smem()] * 3 + [vmem()] * (len(base) + len(parts)),
            out_specs=vmem(),
            out_shape=jax.ShapeDtypeStruct(rows.shape, jnp.float32),
            input_output_aliases={} if first else {3: 0},
            compiler_params=grant(6),
        )(meta, near_tab, far_tab, *base, *parts)
    out = out.reshape(planes, orbs // 8, cells // LANES, 8, LANES).transpose(0, 1, 3, 2, 4)
    return out.reshape(planes, orbs, cells).transpose(1, 0, 2)


def solution(mesh):
    in_specs = (
        P("grp", "slc", None),
        P("grp", "slc", None),
        P("grp", None, None),
        P("grp", None),
        P("grp", None),
        P("grp", None),
        P(),
    )
    return jax.shard_map(operator, mesh=mesh, in_specs=in_specs, out_specs=P("grp", "slc", None), check_vma=False)
```

profile of v0, /device:TPU:7, one launch (start us, length us, event | category | flops | bytes accessed | tf_op | source)
XLA Modules:
  0.0 153.5 jit_solution(16917515456373040274)
XLA Ops:
  1.5 5.8 %all-to-all-start = ((s32[8,1,18]{2,1,0:T(1,128)}), s32[8,1,18]{2,1,0:T(1,128)S(1)}, u32[]{:S(2)}, u32[]{:S(2)}) async-start(s32[8,1,18]{2,1,0:T(1,128)} %bitcast.10), calls=%async_computation | async-start | bytes 8192 | tf_op jit(solution)/shard_map/all_to_all | solution.py:380
  8.2 3.2 %all-to-all-done = s32[8,1,18]{2,1,0:T(1,128)S(1)} async-done(((s32[8,1,18]{2,1,0:T(1,128)}), s32[8,1,18]{2,1,0:T(1,128)S(1)}, u32[]{:S(2)}, u32[]{:S(2)}) %all-to-all-start) | async-done | bytes 608 | tf_op jit(solution)/shard_map/all_to_all | solution.py:380
  11.3 1.2 copy-done
  12.5 2.5 %far_pack.1 = (f32[2,216,128]{2,1,0:T(8,128)S(1)}, f32[2,216,128]{2,1,0:T(8,128)S(1)}, f32[2,216,128]{2,1,0:T(8,128)S(1)}, f32[2,216,128]{2,1,0:T(8,128)S(1)}, f...) custom-call(s32[8,18]{1,0:T(8,128)S(1)} %bitcast.33, ...), custom_call_target="tpu_custom_call" | custom-call | tf_op jit(solution)/shard_map/far_pack/pallas_call | solution.py:401
  15.0 3.0 %collective-permute-start.3 = (f32[2,216,128]{2,1,0:T(8,128)S(1)}, f32[2,216,128]{2,1,0:T(8,128)S(1)}, u32[]{:S(2)}, u32[]{:S(2)}) collective-permute-start(f32[2,216,128]{2,1,0:T(8,128)S(1)} %get-tuple-element.50), channel_id=1, source_target_pairs={{0,0},{1,5},{2,10},{3,15},{4,4},{5,1},{6,14},{7,11},{8,8},{9,13},{... | collective-permute-start | bytes 663560 | tf_op jit(solution)/shard_map/ppermute | solution.py:421
  18.1 2.6 %collective-permute-start.4 = (f32[2,216,128]{2,1,0:T(8,128)S(1)}, f32[2,216,128]{2,1,0:T(8,128)S(1)}, u32[]{:S(2)}, u32[]{:S(2)}) collective-permute-start(f32[2,216,128]{2,1,0:T(8,128)S(1)} %get-tuple-element.51), channel_id=1, source_target_pairs={{0,5},{1,0},{2,15},{3,10},{4,1},{5,4},{6,11},{7,14},{8,13},{9,8},{... | collective-permute-start | bytes 663560 | tf_op jit(solution)/shard_map/ppermute | solution.py:421
  21.5 1.8 %near_pack.1 = (f32[4,216,128]{2,1,0:T(8,128)S(1)}, f32[4,216,128]{2,1,0:T(8,128)S(1)}, f32[4,216,128]{2,1,0:T(8,128)S(1)}, f32[4,216,128]{2,1,0:T(8,128)S(1)}, s32[5,16]{1,0:T(8,128)S(1)}) custom-call(s32[222]{0:T(256)S(1)} %concatenate.9.meta, f32[1728,128]{1,0:T(8,128)S(1)} %bitcast.30), custom_call_target="tpu_custom_call" | custom-call | tf_op jit(solution)/shard_map/near_pack/pallas_call | solution.py:386
  23.5 2.0 %collective-permute-start.2 = (f32[4,216,128]{2,1,0:T(8,128)S(1)}, f32[4,216,128]{2,1,0:T(8,128)S(1)}, u32[]{:S(2)}, u32[]{:S(2)}) collective-permute-start(f32[4,216,128]{2,1,0:T(8,128)S(1)} %get-tuple-element.49), channel_id=1, source_target_pairs={{0,3},{1,2},{2,1},{3,0},{4,7},{5,6},{6,5},{7,4},{8,11},{9,10},{10,... | collective-permute-start | bytes 1327112 | tf_op jit(solution)/shard_map/ppermute | solution.py:400
  26.1 3.8 %collective-permute-done.4.refs_5_ = f32[2,216,128]{2,1,0:T(8,128)S(1)} collective-permute-done((f32[2,216,128]{2,1,0:T(8,128)S(1)}, f32[2,216,128]{2,1,0:T(8,128)S(1)}, u32[]{:S(2)}, u32[]{:S(2)}) %collective-permute-start.4) | collective-permute-done | bytes 221216 | tf_op jit(solution)/shard_map/ppermute | solution.py:421
  30.0 2.8 %collective-permute-done.5.refs_6_ = f32[2,216,128]{2,1,0:T(8,128)S(1)} collective-permute-done((f32[2,216,128]{2,1,0:T(8,128)S(1)}, f32[2,216,128]{2,1,0:T(8,128)S(1)}, u32[]{:S(2)}, u32[]{:S(2)}) %collective-permute-start.5) | collective-permute-done | bytes 221216 | tf_op jit(solution)/shard_map/ppermute | solution.py:421
  32.8 2.3 %collective-permute-start.14 = (f32[2,216,128]{2,1,0:T(8,128)S(1)}, f32[2,216,128]{2,1,0:T(8,128)S(1)}, u32[]{:S(2)}, u32[]{:S(2)}) collective-permute-start(f32[2,216,128]{2,1,0:T(8,128)S(1)} %get-tuple-element.69), channel_id=1, source_target_pairs={{0,16},{1,21},{2,26},{3,31},{4,20},{5,17},{6,30},{7,27},{8,24},{9,... | collective-permute-start | bytes 663560 | tf_op jit(solution)/shard_map/ppermute | solution.py:421
  35.1 16.7 %collective-permute-done.6.refs_7_ = f32[2,216,128]{2,1,0:T(8,128)S(1)} collective-permute-done((f32[2,216,128]{2,1,0:T(8,128)S(1)}, f32[2,216,128]{2,1,0:T(8,128)S(1)}, u32[]{:S(2)}, u32[]{:S(2)}) %collective-permute-start.6) | collective-permute-done | bytes 221216 | tf_op jit(solution)/shard_map/ppermute | solution.py:421
  51.8 4.4 %collective-permute-start.15 = (f32[2,216,128]{2,1,0:T(8,128)S(1)}, f32[2,216,128]{2,1,0:T(8,128)S(1)}, u32[]{:S(2)}, u32[]{:S(2)}) collective-permute-start(f32[2,216,128]{2,1,0:T(8,128)S(1)} %get-tuple-element.70), channel_id=1, source_target_pairs={{0,21},{1,16},{2,31},{3,26},{4,17},{5,20},{6,27},{7,30},{8,29},{9,... | collective-permute-start | bytes 663560 | tf_op jit(solution)/shard_map/ppermute | solution.py:421
  56.2 2.2 %collective-permute-start.16 = (f32[2,216,128]{2,1,0:T(8,128)S(1)}, f32[2,216,128]{2,1,0:T(8,128)S(1)}, u32[]{:S(2)}, u32[]{:S(2)}) collective-permute-start(f32[2,216,128]{2,1,0:T(8,128)S(1)} %get-tuple-element.71), channel_id=1, source_target_pairs={{0,26},{1,31},{2,16},{3,21},{4,30},{5,27},{6,20},{7,17},{8,18},{9,... | collective-permute-start | bytes 663560 | tf_op jit(solution)/shard_map/ppermute | solution.py:421
  58.5 1.1 tables.1
  59.6 1.8 %shard_map.118 = (f32[2,216,128]{2,1,0:T(8,128)S(1)}, f32[2,216,128]{2,1,0:T(8,128)S(1)}, f32[2,216,128]{2,1,0:T(8,128)S(1)}, f32[2,216,128]{2,1,0:T(8,128)S(1)}...) custom-call(s32[222]{0:T(256)S(1)} %concatenate.9.meta, ...), custom_call_target="tpu_custom_call" | custom-call | flops 2000000000 | bytes 8000000 | tf_op jit(solution)/shard_map/pallas_call | solution.py:230
  61.5 10.5 %collective-permute-start.7 = (f32[2,216,128]{2,1,0:T(8,128)S(1)}, f32[2,216,128]{2,1,0:T(8,128)S(1)}, u32[]{:S(2)}, u32[]{:S(2)}) collective-permute-start(f32[2,216,128]{2,1,0:T(8,128)S(1)} %get-tuple-element.61), channel_id=1, source_target_pairs={{0,1},{1,0},{2,3},{3,2},{4,5},{5,4},{6,7},{7,6},{8,9},{9,8},{10,11... | collective-permute-start | bytes 663560 | tf_op jit(solution)/shard_map/ppermute | solution.py:431
  72.0 8.9 %collective-permute-start.9 = (f32[2,216,128]{2,1,0:T(8,128)S(1)}, f32[2,216,128]{2,1,0:T(8,128)S(1)}, u32[]{:S(2)}, u32[]{:S(2)}) collective-permute-start(f32[2,216,128]{2,1,0:T(8,128)S(1)} %get-tuple-element.63), channel_id=1, source_target_pairs={{0,3},{1,2},{2,1},{3,0},{4,7},{5,6},{6,5},{7,4},{8,11},{9,10},{10,... | collective-permute-start | bytes 663560 | tf_op jit(solution)/shard_map/ppermute | solution.py:431
  80.9 7.1 %collective-permute-start.10 = (f32[2,216,128]{2,1,0:T(8,128)S(1)}, f32[2,216,128]{2,1,0:T(8,128)S(1)}, u32[]{:S(2)}, u32[]{:S(2)}) collective-permute-start(f32[2,216,128]{2,1,0:T(8,128)S(1)} %get-tuple-element.64), channel_id=1, source_target_pairs={{0,0},{5,1},{10,2},{15,3},{4,4},{1,5},{14,6},{11,7},{8,8},{13,9},{... | collective-permute-start | bytes 663560 | tf_op jit(solution)/shard_map/ppermute | solution.py:430
  88.0 5.2 %collective-permute-start.11 = (f32[2,216,128]{2,1,0:T(8,128)S(1)}, f32[2,216,128]{2,1,0:T(8,128)S(1)}, u32[]{:S(2)}, u32[]{:S(2)}) collective-permute-start(f32[2,216,128]{2,1,0:T(8,128)S(1)} %get-tuple-element.65), channel_id=1, source_target_pairs={{5,0},{0,1},{15,2},{10,3},{1,4},{4,5},{11,6},{14,7},{13,8},{8,9},{... | collective-permute-start | bytes 663560 | tf_op jit(solution)/shard_map/ppermute | solution.py:430
  93.2 7.0 %shard_map.120 = (f32[2,216,128]{2,1,0:T(8,128)S(1)}, f32[2,216,128]{2,1,0:T(8,128)S(1)}, f32[2,216,128]{2,1,0:T(8,128)S(1)}, f32[2,216,128]{2,1,0:T(8,128)S(1)}...) custom-call(s32[222]{0:T(256)S(1)} %concatenate.9.meta, ...), custom_call_target="tpu_custom_call" | custom-call | flops 2000000000 | bytes 8000000 | tf_op jit(solution)/shard_map/pallas_call | solution.py:230
  100.3 1.5 collective-permute-start.13
  101.8 2.3 %collective-permute-start.18 = (f32[2,216,128]{2,1,0:T(8,128)S(1)}, f32[2,216,128]{2,1,0:T(8,128)S(1)}, u32[]{:S(2)}, u32[]{:S(2)}) collective-permute-start(f32[2,216,128]{2,1,0:T(8,128)S(1)} %get-tuple-element.74), channel_id=1, source_target_pairs={{0,1},{1,0},{2,3},{3,2},{4,5},{5,4},{6,7},{7,6},{8,9},{9,8},{10,11... | collective-permute-start | bytes 663560 | tf_op jit(solution)/shard_map/ppermute | solution.py:431
  104.1 1.7 %collective-permute-start.20 = (f32[2,216,128]{2,1,0:T(8,128)S(1)}, f32[2,216,128]{2,1,0:T(8,128)S(1)}, u32[]{:S(2)}, u32[]{:S(2)}) collective-permute-start(f32[2,216,128]{2,1,0:T(8,128)S(1)} %get-tuple-element.76), channel_id=1, source_target_pairs={{0,3},{1,2},{2,1},{3,0},{4,7},{5,6},{6,5},{7,4},{8,11},{9,10},{10,... | collective-permute-start | bytes 663560 | tf_op jit(solution)/shard_map/ppermute | solution.py:431
  106.1 2.7 %collective-permute-start.21 = (f32[2,216,128]{2,1,0:T(8,128)S(1)}, f32[2,216,128]{2,1,0:T(8,128)S(1)}, u32[]{:S(2)}, u32[]{:S(2)}) collective-permute-start(f32[2,216,128]{2,1,0:T(8,128)S(1)} %get-tuple-element.77), channel_id=1, source_target_pairs={{16,0},{21,1},{26,2},{31,3},{20,4},{17,5},{30,6},{27,7},{24,8},{29... | collective-permute-start | bytes 663560 | tf_op jit(solution)/shard_map/ppermute | solution.py:430
  108.8 8.7 %collective-permute-done.13.refs_8_ = f32[2,216,128]{2,1,0:T(8,128)S(1)} collective-permute-done((f32[2,216,128]{2,1,0:T(8,128)S(1)}, f32[2,216,128]{2,1,0:T(8,128)S(1)}, u32[]{:S(2)}, u32[]{:S(2)}) %collective-permute-start.13) | collective-permute-done | bytes 221216 | tf_op jit(solution)/shard_map/ppermute | solution.py:430
  117.8 4.6 %collective-permute-start.24 = (f32[2,216,128]{2,1,0:T(8,128)S(1)}, f32[2,216,128]{2,1,0:T(8,128)S(1)}, u32[]{:S(2)}, u32[]{:S(2)}) collective-permute-start(f32[2,216,128]{2,1,0:T(8,128)S(1)} %get-tuple-element.80), channel_id=1, source_target_pairs={{31,0},{26,1},{21,2},{16,3},{27,4},{30,5},{17,6},{20,7},{23,8},{18... | collective-permute-start | bytes 663560 | tf_op jit(solution)/shard_map/ppermute | solution.py:430
  122.4 2.0 %shard_map.119.base = f32[1728,128]{1,0:T(8,128)} custom-call(s32[222]{0:T(256)S(1)} %concatenate.9.meta, s32[5,16]{1,0:T(8,128)S(1)} %get-tuple-element.43.tab.near_tab, s32[2,16]{1,0:T(2,128)S(1)} %get-tuple-element.44.far_tab, f32[1728,128]{1,0:T(8,128)S(1)} %bitcast.32, f32[1728,128]{1,0:T(8,128)S(1)} %bitcast.31, ...), custom_call_target="tpu_custom_call" | custom-call | tf_op jit(solution)/shard_map/pallas_call | solution.py:438
  124.4 2.6 %collective-permute-done.22.refs_5_ = f32[2,216,128]{2,1,0:T(8,128)S(1)} collective-permute-done((f32[2,216,128]{2,1,0:T(8,128)S(1)}, f32[2,216,128]{2,1,0:T(8,128)S(1)}, u32[]{:S(2)}, u32[]{:S(2)}) %collective-permute-start.22) | collective-permute-done | bytes 221216 | tf_op jit(solution)/shard_map/ppermute | solution.py:430
  127.1 17.7 %collective-permute-done.23.refs_6_ = f32[2,216,128]{2,1,0:T(8,128)S(1)} collective-permute-done((f32[2,216,128]{2,1,0:T(8,128)S(1)}, f32[2,216,128]{2,1,0:T(8,128)S(1)}, u32[]{:S(2)}, u32[]{:S(2)}) %collective-permute-start.23) | collective-permute-done | bytes 221216 | tf_op jit(solution)/shard_map/ppermute | solution.py:430
  144.8 6.1 %collective-permute-done.24.refs_7_ = f32[2,216,128]{2,1,0:T(8,128)S(1)} collective-permute-done((f32[2,216,128]{2,1,0:T(8,128)S(1)}, f32[2,216,128]{2,1,0:T(8,128)S(1)}, u32[]{:S(2)}, u32[]{:S(2)}) %collective-permute-start.24) | collective-permute-done | bytes 221216 | tf_op jit(solution)/shard_map/ppermute | solution.py:430
  150.9 2.6 %shard_map.121 = f32[1728,128]{1,0:T(8,128)} custom-call(s32[222]{0:T(256)S(1)} %concatenate.9.meta, s32[5,16]{1,0:T(8,128)S(1)} %get-tuple-element.43.tab.near_tab, s32[2,16]{1,0:T(2,128)S(1)} %get-tuple-element.44.far_tab, f32[1728,128]{1,0:T(8,128)} %shard_map.119.base, ...), custom_call_target="tpu_custom_call", output_to_operand_aliasing={{}: (3, {})} | custom-call | tf_op jit(solution)/shard_map/pallas_call | solution.py:438
  (49 shorter events, 4.6 us)
Async XLA Ops:
  0.0 58.4 %copy-start.4 = (f32[48,128]{1,0:T(8,128)S(1)}, f32[48,128]{1,0:T(8,128)}, u32[]{:S(2)}) copy-start(f32[48,128]{1,0:T(8,128)} %constant.19.clone.sine) | copy-start | bytes 73732
  0.0 58.4 %copy-start.3 = (f32[48,384]{1,0:T(8,128)S(1)}, f32[48,384]{1,0:T(8,128)}, u32[]{:S(2)}) copy-start(f32[48,384]{1,0:T(8,128)} %constant.20.clone.wide) | copy-start | bytes 221188
  0.0 58.4 %copy-start.5 = (f32[48,128]{1,0:T(8,128)S(1)}, f32[48,128]{1,0:T(8,128)}, u32[]{:S(2)}) copy-start(f32[48,128]{1,0:T(8,128)} %constant.21.clone.lams) | copy-start | bytes 73732
  1.5 9.9 %all-to-all-start = ((s32[8,1,18]{2,1,0:T(1,128)}), s32[8,1,18]{2,1,0:T(1,128)S(1)}, u32[]{:S(2)}, u32[]{:S(2)}) async-start(s32[8,1,18]{2,1,0:T(1,128)} %bitcast.10), calls=%async_computation | async-start | bytes 8192 | tf_op jit(solution)/shard_map/all_to_all | solution.py:380
  12.5 9.0 %copy-start.1 = (f32[8,12,2304]{2,0,1:T(8,128)S(1)}, f32[8,12,2304]{2,0,1:T(8,128)}, u32[]{:S(2)}) copy-start(f32[8,12,2304]{2,0,1:T(8,128)} %param.12) | copy-start | bytes 2654212
  12.5 47.1 %copy-start.6 = (s32[36,128]{1,0:T(8,128)S(1)}, s32[36,128]{1,0:T(8,128)}, u32[]{:S(2)}) copy-start(s32[36,128]{1,0:T(8,128)} %constant.22.clone.refs_14_) | copy-start | bytes 55300
  15.0 10.5 %collective-permute-start.3 = (f32[2,216,128]{2,1,0:T(8,128)S(1)}, f32[2,216,128]{2,1,0:T(8,128)S(1)}, u32[]{:S(2)}, u32[]{:S(2)}) collective-permute-start(f32[2,216,128]{2,1,0:T(8,128)S(1)} %get-tuple-element.50), channel_id=1, source_target_pairs={{0,0},{1,5},{2,10},{3,15},{4,4},{5,1},{6,14},{7,11},{8,8},{9,13},{... | collective-permute-start | bytes 663560 | tf_op jit(solution)/shard_map/ppermute | solution.py:421
  18.1 11.9 %collective-permute-start.4 = (f32[2,216,128]{2,1,0:T(8,128)S(1)}, f32[2,216,128]{2,1,0:T(8,128)S(1)}, u32[]{:S(2)}, u32[]{:S(2)}) collective-permute-start(f32[2,216,128]{2,1,0:T(8,128)S(1)} %get-tuple-element.51), channel_id=1, source_target_pairs={{0,5},{1,0},{2,15},{3,10},{4,1},{5,4},{6,11},{7,14},{8,13},{9,8},{... | collective-permute-start | bytes 663560 | tf_op jit(solution)/shard_map/ppermute | solution.py:421
  23.3 32.9 %collective-permute-start = (f32[4,216,128]{2,1,0:T(8,128)S(1)}, f32[4,216,128]{2,1,0:T(8,128)S(1)}, u32[]{:S(2)}, u32[]{:S(2)}) collective-permute-start(f32[4,216,128]{2,1,0:T(8,128)S(1)} %get-tuple-element.47), channel_id=1, source_target_pairs={{0,1},{1,0},{2,3},{3,2},{4,5},{5,4},{6,7},{7,6},{8,9},{9,8},{10,11... | collective-permute-start | bytes 1327112 | tf_op jit(solution)/shard_map/ppermute | solution.py:400
  23.4 36.2 %collective-permute-start.1 = (f32[4,216,128]{2,1,0:T(8,128)S(1)}, f32[4,216,128]{2,1,0:T(8,128)S(1)}, u32[]{:S(2)}, u32[]{:S(2)}) collective-permute-start(f32[4,216,128]{2,1,0:T(8,128)S(1)} %get-tuple-element.48), channel_id=1, source_target_pairs={{0,2},{1,3},{2,0},{3,1},{4,6},{5,7},{6,4},{7,5},{8,10},{9,11},{10,... | collective-permute-start | bytes 1327112 | tf_op jit(solution)/shard_map/ppermute | solution.py:400
  23.5 36.1 %collective-permute-start.2 = (f32[4,216,128]{2,1,0:T(8,128)S(1)}, f32[4,216,128]{2,1,0:T(8,128)S(1)}, u32[]{:S(2)}, u32[]{:S(2)}) collective-permute-start(f32[4,216,128]{2,1,0:T(8,128)S(1)} %get-tuple-element.49), channel_id=1, source_target_pairs={{0,3},{1,2},{2,1},{3,0},{4,7},{5,6},{6,5},{7,4},{8,11},{9,10},{10,... | collective-permute-start | bytes 1327112 | tf_op jit(solution)/shard_map/ppermute | solution.py:400
  25.5 7.3 %collective-permute-start.5 = (f32[2,216,128]{2,1,0:T(8,128)S(1)}, f32[2,216,128]{2,1,0:T(8,128)S(1)}, u32[]{:S(2)}, u32[]{:S(2)}) collective-permute-start(f32[2,216,128]{2,1,0:T(8,128)S(1)} %get-tuple-element.52), channel_id=1, source_target_pairs={{0,10},{1,15},{2,0},{3,5},{4,14},{5,11},{6,4},{7,1},{8,2},{9,7},{1... | collective-permute-start | bytes 663560 | tf_op jit(solution)/shard_map/ppermute | solution.py:421
  30.0 21.8 %collective-permute-start.6 = (f32[2,216,128]{2,1,0:T(8,128)S(1)}, f32[2,216,128]{2,1,0:T(8,128)S(1)}, u32[]{:S(2)}, u32[]{:S(2)}) collective-permute-start(f32[2,216,128]{2,1,0:T(8,128)S(1)} %get-tuple-element.53), channel_id=1, source_target_pairs={{0,15},{1,10},{2,5},{3,0},{4,11},{5,14},{6,1},{7,4},{8,7},{9,2},{1... | collective-permute-start | bytes 663560 | tf_op jit(solution)/shard_map/ppermute | solution.py:421
  32.8 39.2 %collective-permute-start.14 = (f32[2,216,128]{2,1,0:T(8,128)S(1)}, f32[2,216,128]{2,1,0:T(8,128)S(1)}, u32[]{:S(2)}, u32[]{:S(2)}) collective-permute-start(f32[2,216,128]{2,1,0:T(8,128)S(1)} %get-tuple-element.69), channel_id=1, source_target_pairs={{0,16},{1,21},{2,26},{3,31},{4,20},{5,17},{6,30},{7,27},{8,24},{9,... | collective-permute-start | bytes 663560 | tf_op jit(solution)/shard_map/ppermute | solution.py:421
  51.8 20.2 %collective-permute-start.15 = (f32[2,216,128]{2,1,0:T(8,128)S(1)}, f32[2,216,128]{2,1,0:T(8,128)S(1)}, u32[]{:S(2)}, u32[]{:S(2)}) collective-permute-start(f32[2,216,128]{2,1,0:T(8,128)S(1)} %get-tuple-element.70), channel_id=1, source_target_pairs={{0,21},{1,16},{2,31},{3,26},{4,17},{5,20},{6,27},{7,30},{8,29},{9,... | collective-permute-start | bytes 663560 | tf_op jit(solution)/shard_map/ppermute | solution.py:421
  56.2 24.7 %collective-permute-start.16 = (f32[2,216,128]{2,1,0:T(8,128)S(1)}, f32[2,216,128]{2,1,0:T(8,128)S(1)}, u32[]{:S(2)}, u32[]{:S(2)}) collective-permute-start(f32[2,216,128]{2,1,0:T(8,128)S(1)} %get-tuple-element.71), channel_id=1, source_target_pairs={{0,26},{1,31},{2,16},{3,21},{4,30},{5,27},{6,20},{7,17},{8,18},{9,... | collective-permute-start | bytes 663560 | tf_op jit(solution)/shard_map/ppermute | solution.py:421
  59.5 28.5 %collective-permute-start.17 = (f32[2,216,128]{2,1,0:T(8,128)S(1)}, f32[2,216,128]{2,1,0:T(8,128)S(1)}, u32[]{:S(2)}, u32[]{:S(2)}) collective-permute-start(f32[2,216,128]{2,1,0:T(8,128)S(1)} %get-tuple-element.72), channel_id=1, source_target_pairs={{0,31},{1,26},{2,21},{3,16},{4,27},{5,30},{6,17},{7,20},{8,23},{9,... | collective-permute-start | bytes 663560 | tf_op jit(solution)/shard_map/ppermute | solution.py:421
  61.5 38.8 %collective-permute-start.7 = (f32[2,216,128]{2,1,0:T(8,128)S(1)}, f32[2,216,128]{2,1,0:T(8,128)S(1)}, u32[]{:S(2)}, u32[]{:S(2)}) collective-permute-start(f32[2,216,128]{2,1,0:T(8,128)S(1)} %get-tuple-element.61), channel_id=1, source_target_pairs={{0,1},{1,0},{2,3},{3,2},{4,5},{5,4},{6,7},{7,6},{8,9},{9,8},{10,11... | collective-permute-start | bytes 663560 | tf_op jit(solution)/shard_map/ppermute | solution.py:431
  72.0 28.3 %collective-permute-start.8 = (f32[2,216,128]{2,1,0:T(8,128)S(1)}, f32[2,216,128]{2,1,0:T(8,128)S(1)}, u32[]{:S(2)}, u32[]{:S(2)}) collective-permute-start(f32[2,216,128]{2,1,0:T(8,128)S(1)} %get-tuple-element.62), channel_id=1, source_target_pairs={{0,2},{1,3},{2,0},{3,1},{4,6},{5,7},{6,4},{7,5},{8,10},{9,11},{10,... | collective-permute-start | bytes 663560 | tf_op jit(solution)/shard_map/ppermute | solution.py:431
  72.0 29.8 %collective-permute-start.9 = (f32[2,216,128]{2,1,0:T(8,128)S(1)}, f32[2,216,128]{2,1,0:T(8,128)S(1)}, u32[]{:S(2)}, u32[]{:S(2)}) collective-permute-start(f32[2,216,128]{2,1,0:T(8,128)S(1)} %get-tuple-element.63), channel_id=1, source_target_pairs={{0,3},{1,2},{2,1},{3,0},{4,7},{5,6},{6,5},{7,4},{8,11},{9,10},{10,... | collective-permute-start | bytes 663560 | tf_op jit(solution)/shard_map/ppermute | solution.py:431
  80.9 23.2 %collective-permute-start.10 = (f32[2,216,128]{2,1,0:T(8,128)S(1)}, f32[2,216,128]{2,1,0:T(8,128)S(1)}, u32[]{:S(2)}, u32[]{:S(2)}) collective-permute-start(f32[2,216,128]{2,1,0:T(8,128)S(1)} %get-tuple-element.64), channel_id=1, source_target_pairs={{0,0},{5,1},{10,2},{15,3},{4,4},{1,5},{14,6},{11,7},{8,8},{13,9},{... | collective-permute-start | bytes 663560 | tf_op jit(solution)/shard_map/ppermute | solution.py:430
  88.0 16.1 %collective-permute-start.11 = (f32[2,216,128]{2,1,0:T(8,128)S(1)}, f32[2,216,128]{2,1,0:T(8,128)S(1)}, u32[]{:S(2)}, u32[]{:S(2)}) collective-permute-start(f32[2,216,128]{2,1,0:T(8,128)S(1)} %get-tuple-element.65), channel_id=1, source_target_pairs={{5,0},{0,1},{15,2},{10,3},{1,4},{4,5},{11,6},{14,7},{13,8},{8,9},{... | collective-permute-start | bytes 663560 | tf_op jit(solution)/shard_map/ppermute | solution.py:430
  93.2 29.2 %copy-start.2 = (f32[8,12,2304]{2,0,1:T(8,128)S(1)}, f32[8,12,2304]{2,0,1:T(8,128)}, u32[]{:S(2)}) copy-start(f32[8,12,2304]{2,0,1:T(8,128)} %param.13) | copy-start | bytes 2654212
  100.3 5.8 %collective-permute-start.12 = (f32[2,216,128]{2,1,0:T(8,128)S(1)}, f32[2,216,128]{2,1,0:T(8,128)S(1)}, u32[]{:S(2)}, u32[]{:S(2)}) collective-permute-start(f32[2,216,128]{2,1,0:T(8,128)S(1)} %get-tuple-element.66), channel_id=1, source_target_pairs={{10,0},{15,1},{0,2},{5,3},{14,4},{11,5},{4,6},{1,7},{2,8},{7,9},{8... | collective-permute-start | bytes 663560 | tf_op jit(solution)/shard_map/ppermute | solution.py:430
  100.3 17.2 %collective-permute-start.13 = (f32[2,216,128]{2,1,0:T(8,128)S(1)}, f32[2,216,128]{2,1,0:T(8,128)S(1)}, u32[]{:S(2)}, u32[]{:S(2)}) collective-permute-start(f32[2,216,128]{2,1,0:T(8,128)S(1)} %get-tuple-element.67), channel_id=1, source_target_pairs={{15,0},{10,1},{5,2},{0,3},{11,4},{14,5},{1,6},{4,7},{7,8},{2,9},{1... | collective-permute-start | bytes 663560 | tf_op jit(solution)/shard_map/ppermute | solution.py:430
  101.8 15.7 %collective-permute-start.18 = (f32[2,216,128]{2,1,0:T(8,128)S(1)}, f32[2,216,128]{2,1,0:T(8,128)S(1)}, u32[]{:S(2)}, u32[]{:S(2)}) collective-permute-start(f32[2,216,128]{2,1,0:T(8,128)S(1)} %get-tuple-element.74), channel_id=1, source_target_pairs={{0,1},{1,0},{2,3},{3,2},{4,5},{5,4},{6,7},{7,6},{8,9},{9,8},{10,11... | collective-permute-start | bytes 663560 | tf_op jit(solution)/shard_map/ppermute | solution.py:431
  104.1 13.7 %collective-permute-start.19 = (f32[2,216,128]{2,1,0:T(8,128)S(1)}, f32[2,216,128]{2,1,0:T(8,128)S(1)}, u32[]{:S(2)}, u32[]{:S(2)}) collective-permute-start(f32[2,216,128]{2,1,0:T(8,128)S(1)} %get-tuple-element.75), channel_id=1, source_target_pairs={{0,2},{1,3},{2,0},{3,1},{4,6},{5,7},{6,4},{7,5},{8,10},{9,11},{10,... | collective-permute-start | bytes 663560 | tf_op jit(solution)/shard_map/ppermute | solution.py:431
  104.1 20.3 %collective-permute-start.20 = (f32[2,216,128]{2,1,0:T(8,128)S(1)}, f32[2,216,128]{2,1,0:T(8,128)S(1)}, u32[]{:S(2)}, u32[]{:S(2)}) collective-permute-start(f32[2,216,128]{2,1,0:T(8,128)S(1)} %get-tuple-element.76), channel_id=1, source_target_pairs={{0,3},{1,2},{2,1},{3,0},{4,7},{5,6},{6,5},{7,4},{8,11},{9,10},{10,... | collective-permute-start | bytes 663560 | tf_op jit(solution)/shard_map/ppermute | solution.py:431
  106.1 18.3 %collective-permute-start.21 = (f32[2,216,128]{2,1,0:T(8,128)S(1)}, f32[2,216,128]{2,1,0:T(8,128)S(1)}, u32[]{:S(2)}, u32[]{:S(2)}) collective-permute-start(f32[2,216,128]{2,1,0:T(8,128)S(1)} %get-tuple-element.77), channel_id=1, source_target_pairs={{16,0},{21,1},{26,2},{31,3},{20,4},{17,5},{30,6},{27,7},{24,8},{29... | collective-permute-start | bytes 663560 | tf_op jit(solution)/shard_map/ppermute | solution.py:430
  117.5 9.5 %collective-permute-start.22 = (f32[2,216,128]{2,1,0:T(8,128)S(1)}, f32[2,216,128]{2,1,0:T(8,128)S(1)}, u32[]{:S(2)}, u32[]{:S(2)}) collective-permute-start(f32[2,216,128]{2,1,0:T(8,128)S(1)} %get-tuple-element.78), channel_id=1, source_target_pairs={{21,0},{16,1},{31,2},{26,3},{17,4},{20,5},{27,6},{30,7},{29,8},{24... | collective-permute-start | bytes 663560 | tf_op jit(solution)/shard_map/ppermute | solution.py:430
  117.5 27.3 %collective-permute-start.23 = (f32[2,216,128]{2,1,0:T(8,128)S(1)}, f32[2,216,128]{2,1,0:T(8,128)S(1)}, u32[]{:S(2)}, u32[]{:S(2)}) collective-permute-start(f32[2,216,128]{2,1,0:T(8,128)S(1)} %get-tuple-element.79), channel_id=1, source_target_pairs={{26,0},{31,1},{16,2},{21,3},{30,4},{27,5},{20,6},{17,7},{18,8},{23... | collective-permute-start | bytes 663560 | tf_op jit(solution)/shard_map/ppermute | solution.py:430
  117.8 33.1 %collective-permute-start.24 = (f32[2,216,128]{2,1,0:T(8,128)S(1)}, f32[2,216,128]{2,1,0:T(8,128)S(1)}, u32[]{:S(2)}, u32[]{:S(2)}) collective-permute-start(f32[2,216,128]{2,1,0:T(8,128)S(1)} %get-tuple-element.80), channel_id=1, source_target_pairs={{31,0},{26,1},{21,2},{16,3},{27,4},{30,5},{17,6},{20,7},{23,8},{18... | collective-permute-start | bytes 663560 | tf_op jit(solution)/shard_map/ppermute | solution.py:430
  (1 other events, 1.2 us)
where the time goes:
time: 154 us; the launch traced here: 153 us
  starting transfers between devices  68 us (44%)
  waiting for transfers between devices  62.1 us (40%)
  Pallas kernels  18.8 us (12%)
  local copies, waits for them, and re-layouts  2.88 us (2%)
    ppermute x8, waiting for transfers between devices, operator(): far_back[q, k] = lax.ppermute(far_out[k], ('grp', 'slc'), back)  35.5 us
    ppermute x6, starting transfers between devices, operator(): lax.ppermute(near_out[k], 'slc', across[k])  23.4 us
    ppermute x8, waiting for transfers between devices, operator(): lax.ppermute(sends[q * slices + k], ('grp', 'slc'), there(q, k))  23.4 us
    ppermute x8, starting transfers between devices, operator(): far_back[q, k] = lax.ppermute(far_out[k], ('grp', 'slc'), back)  21.3 us
    ppermute x8, starting transfers between devices, operator(): lax.ppermute(sends[q * slices + k], ('grp', 'slc'), there(q, k))  15.3 us
    pallas_call x2, Pallas kernels, pair_call(): pl.pallas_call(functools.partial(pair_kernel, slices, slab, round_id), in...  8.88 us
    all_to_all x1, starting transfers between devices, operator(): lists = lax.all_to_all(mine, 'grp', 0, 0, tiled=True)  5.78 us
    pallas_call x2, Pallas kernels, operator(): pl.pallas_call(functools.partial(sum_kernel, slices, orbs, planes, chosen...  4.58 us
  transfers between devices with their start and end apart: 26, of which 9 were waited for; matrix products, arithmetic and copies ran while one was open for 1% of the time, Pallas kernels for 9%

commit v1 on v0

--- a/solution.py
+++ b/solution.py
@@ -63,7 +63,8 @@
     for b in range(ROWS_BLK):
         part = jnp.where((lane >= b * B) & (lane < (b + 1) * B), w, 0.0)
         ph, plo = split(part)
-        inv_h[b * LANES : (b + 1) * LANES, :] = ph
+        half = ph[: LANES // 2]
+        inv_h[b * LANES : (b + 1) * LANES, :] = jnp.concatenate([half, half], axis=0)
         inv_l[b * LANES : (b + 1) * LANES, :] = plo
     pair = lams[...]
     for k, lam in enumerate(lam_np()):
@@ -98,7 +99,7 @@
     )(jnp.asarray(padded), jnp.asarray(wide), jnp.asarray(lams), after)
 
 
-def one_slot(near, box, shifted, left_h, left_l, mid, mid2, inv_lh, inv_ll, sine3, fwd_h, fwd_l, inv_h, inv_l, weight, spots, out, e0, e1, e2):
+def one_slot(near, box, shifted, left_h, left_l, mid, mid2, inv_left, sine3, fwd_h, fwd_l, inv_h, inv_l, weight, spots, out, e0, e1, e2):
     lane = lax.broadcasted_iota(jnp.int32, (B, LANES), 1)
 
     def turned(source, d0, d1, d2, j_list):
@@ -141,7 +142,7 @@
             for h in range(2):
                 b = ROWS_BLK * m + 2 * p + h
                 mid[pl.ds(b, B, stride=PITCH), :] = y[m * B : (m + 1) * B, h * LANES : (h + 1) * LANES]
-    group = 6
+    group = 48
 
     def second(i, carry):
         first = i * group
@@ -158,13 +159,14 @@
     for m in range(NBLK):
         for b in range(ROWS_BLK):
             start = (ROWS_BLK * m + b) * PITCH
-            zh, zl = split(mid2[start : start + B, :])
-            inv_lh[m * B : (m + 1) * B, b * LANES : (b + 1) * LANES] = zh
-            inv_ll[m * B : (m + 1) * B, b * LANES : (b + 1) * LANES] = zl
+            z = mid2[start : start + B, :]
+            zh = z.astype(jnp.bfloat16).astype(jnp.float32)
+            both = zh + pltpu.roll(z - zh, LANES // 2, axis=1)
+            inv_left[m * B : (m + 1) * B, b * LANES : (b + 1) * LANES] = both.astype(jnp.bfloat16)
     ka = slice(0, 6 * LANES)
     kb = slice(5 * LANES, 8 * LANES)
-    ya = mm3(inv_lh[:, ka], inv_ll[:, ka], inv_h[ka, : 2 * LANES], inv_l[ka, : 2 * LANES])
-    yb = mm3(inv_lh[:, kb], inv_ll[:, kb], inv_h[kb, 2 * LANES :], inv_l[kb, 2 * LANES :])
+    ya = mm(inv_left[:, ka], inv_h[ka, : 2 * LANES]) + mm(inv_left[:, ka], inv_l[ka, : 2 * LANES])
+    yb = mm(inv_left[:, kb], inv_h[kb, 2 * LANES :]) + mm(inv_left[:, kb], inv_l[kb, 2 * LANES :])
     for m in range(NBLK):
         y = jnp.concatenate([ya[m * B : (m + 1) * B], yb[m * B : (m + 1) * B]], axis=1)
         pot = along_first(y)
@@ -179,33 +181,33 @@
             out[1, pl.ds(j, B, stride=COLS), :] = part
 
 
-def pair_kernel(slices, slab, round_id, meta, tab, after, *refs):
+def pair_kernel(slices, slab, round_id, ranks, tab, *refs):
     nears, refs = refs[:slices], refs[slices:]
     fars, refs = refs[:slices], refs[slices:]
     consts, refs = refs[:7], refs[7:]
+    if ranks[0]:
+        refs = refs[slices:]
     near_outs, refs = refs[:slices], refs[slices:]
     far_outs, refs = refs[:slices], refs[slices:]
-    token, refs = refs[0], refs[1:]
-    token[0] = after[0]
-    near, box, shifted, left_h, left_l, mid, mid2, inv_lh, inv_ll, out = refs
-    own = meta[1]
+    near, box, shifted, left_h, left_l, mid, mid2, inv_left, out = refs
+    own = tab[5, 0]
     zeros = jnp.zeros((PAD, LANES), jnp.float32)
     box[:PAD, :] = zeros
     box[PAD + BOX :, :] = zeros
-    for c in range(CAP):
+    for at, c in enumerate(ranks):
         slot = (round_id * slices + own) * CAP + c
 
         @pl.when(tab[0, slot] > 0)
         def _():
             for k in range(slices):
                 start = (own ^ k) * slab
-                near[pl.ds(start, slab), :] = nears[k][round_id * CAP + c]
+                near[pl.ds(start, slab), :] = nears[k][c]
                 box[pl.ds(PAD + start, slab), :] = fars[k][c]
-            one_slot(near, box, shifted, left_h, left_l, mid, mid2, inv_lh, inv_ll, *consts, out, tab[2, slot], tab[3, slot], tab[4, slot])
+            one_slot(near, box, shifted, left_h, left_l, mid, mid2, inv_left, *consts, out, tab[2, slot], tab[3, slot], tab[4, slot])
             for k in range(slices):
                 start = (own ^ k) * slab
                 near_outs[k][c] = out[0, pl.ds(start, slab), :]
-                far_outs[k][c] = out[1, pl.ds(start, slab), :]
+                far_outs[k][at] = out[1, pl.ds(start, slab), :]
 
 
 def kept(x):
@@ -224,14 +226,17 @@
     return pl.BlockSpec(memory_space=pltpu.VMEM)
 
 
-def pair_call(slices, slab, round_id, meta, tab, after, nears, fars, consts):
+def pair_call(slices, slab, round_id, ranks, tab, nears, fars, consts, earlier):
     spots = np.arange(B * B).reshape(COLS, LANES)
     spots = jnp.asarray(np.concatenate([spots // B, spots % B]).astype(np.int32))
+    operands = [tab, *map(kept, nears), *map(kept, fars), *map(kept, consts), spots, *map(kept, earlier)]
     outs = pl.pallas_call(
-        functools.partial(pair_kernel, slices, slab, round_id),
-        in_specs=[smem()] * 3 + [vmem()] * (2 * slices + 7),
-        out_specs=[vmem()] * (2 * slices) + [smem()],
-        out_shape=[pltpu.VMEM((CAP, slab, LANES), jnp.float32)] * (2 * slices) + [jax.ShapeDtypeStruct((1,), jnp.int32)],
+        functools.partial(pair_kernel, slices, slab, round_id, ranks),
+        in_specs=[smem()] + [vmem()] * (len(operands) - 1),
+        out_specs=[vmem()] * (2 * slices),
+        out_shape=[pltpu.VMEM((CAP, slab, LANES), jnp.float32)] * slices
+        + [pltpu.VMEM((len(ranks), slab, LANES), jnp.float32)] * slices,
+        input_output_aliases={len(operands) - len(earlier) + k: k for k in range(len(earlier))},
         scratch_shapes=[
             pltpu.VMEM((BOX, LANES), jnp.float32),
             pltpu.VMEM((BOX + 2 * PAD, LANES), jnp.float32),
@@ -241,13 +246,12 @@
             pltpu.VMEM((B * PITCH, LANES), jnp.float32),
             pltpu.VMEM((B * PITCH, LANES), jnp.float32),
             pltpu.VMEM((NBLK * B, ROWS_BLK * LANES), jnp.bfloat16),
-            pltpu.VMEM((NBLK * B, ROWS_BLK * LANES), jnp.bfloat16),
             pltpu.VMEM((2, BOX, LANES), jnp.float32),
         ],
         cost_estimate=pl.CostEstimate(flops=2 * 10**9, transcendentals=0, bytes_accessed=8 * 10**6),
         compiler_params=grant(24),
-    )(meta, tab, after, *map(kept, nears), *map(kept, fars), *map(kept, consts), spots)
-    return outs[:slices], outs[slices : 2 * slices], outs[-1]
+    )(*operands)
+    return outs[:slices], outs[slices:]
 
 
 def slab_pieces(orbs, planes, o):
@@ -259,9 +263,11 @@
 
 
 def near_kernel(groups, slices, listed, orbs, planes, meta, values, *refs):
-    outs, (tab, seen) = refs[:slices], refs[slices:]
+    rounds = groups // slices
+    outs, (tab, seen) = refs[: rounds * slices], refs[rounds * slices :]
     gid = meta[0]
     own = meta[1]
+    tab[5, 0] = own
     owner_at, remote_at, resident_at, count_at = 2, 2 + listed, 2 + 2 * listed, 2 + 3 * listed
     offset_at = count_at + slices
     for g in range(groups):
@@ -289,15 +295,15 @@
         return carry
 
     lax.fori_loop(0, listed, place, 0)
-    for k in range(slices):
-        for q in range(groups // slices):
+    for q in range(rounds):
+        for k in range(slices):
             for c in range(CAP):
                 n = (q * slices + (own ^ k)) * CAP + c
 
                 @pl.when(tab[0, n] > 0)
                 def _():
                     for start, count, to in slab_pieces(orbs, planes, tab[1, n]):
-                        outs[k][q * CAP + c, to : to + count, :] = values[pl.ds(start, count, stride=8), :]
+                        outs[q * slices + k][c, to : to + count, :] = values[pl.ds(start, count, stride=8), :]
 
 
 def far_kernel(groups, slices, listed, orbs, planes, lists, values, *refs):
@@ -334,24 +340,22 @@
                         outs[q * slices + k][c, to : to + count, :] = values[pl.ds(start, count, stride=8), :]
 
 
-def sum_kernel(slices, orbs, planes, rounds, first, meta, near_tab, far_tab, base, *refs):
+def sum_kernel(slices, orbs, planes, near_keys, far_keys, first, near_tab, far_tab, base, *refs):
     if first:
         values, refs = refs[0], refs[1:]
-    count = len(rounds) * slices
-    nears, fars, out = refs[:count], refs[count : 2 * count], refs[-1]
-    own = meta[1]
+    out = refs[-1]
+    own = near_tab[5, 0]
     out[...] = base[...] * values[...] if first else base[...]
-    for tab, parts in ((near_tab, nears), (far_tab, fars)):
-        for at, q in enumerate(rounds):
-            for k in range(slices):
-                for c in range(CAP):
-                    n = (q * slices + (own ^ k)) * CAP + c
-
-                    @pl.when(tab[0, n] > 0)
-                    def _():
-                        for start, count, to in slab_pieces(orbs, planes, tab[1, n]):
-                            rows = pl.ds(start, count, stride=8)
-                            out[rows, :] = out[rows, :] - parts[at * slices + k][c, to : to + count, :]
+    for tab, keys, parts in ((near_tab, near_keys, refs), (far_tab, far_keys, refs[len(near_keys) :])):
+        for part, (q, k, ranks) in zip(parts, keys):
+            for at, c in enumerate(ranks):
+                n = (q * slices + (own ^ k)) * CAP + c
+
+                @pl.when(tab[0, n] > 0)
+                def _():
+                    for start, count, to in slab_pieces(orbs, planes, tab[1, n]):
+                        rows = pl.ds(start, count, stride=8)
+                        out[rows, :] = out[rows, :] - part[at, to : to + count, :]
 
 
 def as_rows(x):
@@ -386,18 +390,20 @@
     packed = pl.pallas_call(
         functools.partial(near_kernel, *sizes),
         in_specs=[smem(), vmem()],
-        out_specs=[vmem()] * slices + [smem()],
-        out_shape=[pltpu.VMEM((rounds * CAP, slab, LANES), jnp.float32)] * slices
-        + [jax.ShapeDtypeStruct((5, groups * CAP), jnp.int32)],
+        out_specs=[vmem()] * len(keys) + [smem()],
+        out_shape=[pltpu.VMEM((CAP, slab, LANES), jnp.float32)] * len(keys)
+        + [jax.ShapeDtypeStruct((6, groups * CAP), jnp.int32)],
         scratch_shapes=[pltpu.SMEM((groups,), jnp.int32)],
         compiler_params=grant(4),
         name="near_pack",
     )(meta, rows)
-    near_tab = packed[slices]
+    near_tab = packed[-1]
     across = [[(s, s ^ k) for s in range(slices)] for k in range(slices)]
-    nears = [packed[0]]
-    for k in range(1, slices):
-        nears.append(lax.ppermute(packed[k], "slc", across[k]))
+    nears = {}
+    for q, k in keys:
+        nears[q, k] = packed[q * slices + k]
+        if k:
+            nears[q, k] = lax.ppermute(nears[q, k], "slc", across[k])
     sends = pl.pallas_call(
         functools.partial(far_kernel, *sizes),
         in_specs=[smem(), vmem()],
@@ -420,31 +426,41 @@
     for q, k in keys:
         fars[q, k] = lax.ppermute(sends[q * slices + k], ("grp", "slc"), there(q, k))
     consts = make_tables(after)
+    every = tuple(range(CAP))
     near_back, far_back = {}, {}
     for q in range(rounds):
-        near_out, far_out, after = pair_call(
-            slices, slab, q, meta, near_tab, after, nears, [fars[q, k] for k in range(slices)], consts
-        )
+        earlier = []
+        for ranks in rank_sets(q, rounds):
+            earlier, far_out = pair_call(
+                slices, slab, q, ranks, near_tab, [nears[q, k] for k in range(slices)],
+                [fars[q, k] for k in range(slices)], consts, earlier
+            )
+            for k in range(slices):
+                back = [(d, s) for s, d in there(q, k)]
+                far_back[q, k, ranks] = lax.ppermute(far_out[k], ("grp", "slc"), back)
         for k in range(slices):
-            back = [(d, s) for s, d in there(q, k)]
-            far_back[q, k] = lax.ppermute(far_out[k], ("grp", "slc"), back)
-            near_back[q, k] = near_out[k] if k == 0 else lax.ppermute(near_out[k], "slc", across[k])
+            near_back[q, k, every] = earlier[k] if k == 0 else lax.ppermute(earlier[k], "slc", across[k])
     out = None
     for chosen in (tuple(range(rounds - 1)), (rounds - 1,)):
         first = out is None
         base = [pot_rows, rows] if first else [out]
-        part = [x for x in keys if x[0] in chosen]
-        parts = [kept(near_back[x]) for x in part] + [kept(far_back[x]) for x in part]
+        near_keys = [x for x in near_back if x[0] in chosen]
+        far_keys = [x for x in far_back if x[0] in chosen]
+        parts = [kept(near_back[x]) for x in near_keys] + [kept(far_back[x]) for x in far_keys]
         out = pl.pallas_call(
-            functools.partial(sum_kernel, slices, orbs, planes, chosen, first),
-            in_specs=[smem()] * 3 + [vmem()] * (len(base) + len(parts)),
+            functools.partial(sum_kernel, slices, orbs, planes, near_keys, far_keys, first),
+            in_specs=[smem()] * 2 + [vmem()] * (len(base) + len(parts)),
             out_specs=vmem(),
             out_shape=jax.ShapeDtypeStruct(rows.shape, jnp.float32),
-            input_output_aliases={} if first else {3: 0},
+            input_output_aliases={} if first else {2: 0},
             compiler_params=grant(6),
-        )(meta, near_tab, far_tab, *base, *parts)
+        )(near_tab, far_tab, *base, *parts)
     out = out.reshape(planes, orbs // 8, cells // LANES, 8, LANES).transpose(0, 1, 3, 2, 4)
     return out.reshape(planes, orbs, cells).transpose(1, 0, 2)
+
+
+def rank_sets(q, rounds):
+    return [(c,) for c in range(CAP)] if q == rounds - 1 else [tuple(range(CAP))]
 
 
 def solution(mesh):

time: 154 us -> 138 us (0.90)
  the two profiles are of different devices: /device:TPU:7 before, /device:TPU:0 now
where the time goes in v1:
time: 138 us; the launch traced here: 137 us
  waiting for transfers between devices  64.6 us (47%)
  starting transfers between devices  50.1 us (36%)
  Pallas kernels  18.1 us (13%)
  local copies, waits for them, and re-layouts  2.92 us (2%)
  other arithmetic  1.42 us (1%)
    ppermute x8, waiting for transfers between devices, operator(): lax.ppermute(sends[q * slices + k], ('grp', 'slc'), there(q, k))  29.7 us
    ppermute x12, waiting for transfers between devices, operator(): far_back[q, k, ranks] = lax.ppermute(far_out[k], ('grp', 'slc'), back)  24.7 us
    ppermute x12, starting transfers between devices, operator(): far_back[q, k, ranks] = lax.ppermute(far_out[k], ('grp', 'slc'), back)  15.2 us
    ppermute x8, starting transfers between devices, operator(): lax.ppermute(sends[q * slices + k], ('grp', 'slc'), there(q, k))  13.4 us
    ppermute x6, starting transfers between devices, operator(): lax.ppermute(earlier[k], 'slc', across[k])  10.9 us
    pallas_call x3, Pallas kernels, pair_call(): pl.pallas_call(functools.partial(pair_kernel, slices, slab, round_id, ran...  8.32 us
    all_to_all x1, starting transfers between devices, operator(): lists = lax.all_to_all(mine, 'grp', 0, 0, tiled=True)  6.03 us
    all_to_all x1, waiting for transfers between devices, operator(): lists = lax.all_to_all(mine, 'grp', 0, 0, tiled=True)  5.55 us
  transfers between devices with their start and end apart: 33, of which 17 were waited for; matrix products, arithmetic and copies ran while one was open for 1% of the time, Pallas kernels for 10%

profile of v1, /device:TPU:0, one launch (start us, length us, event | category | flops | bytes accessed | tf_op | source)
XLA Modules:
  0.0 137.3 jit_solution(5683068732845491329)
XLA Ops:
  2.9 1.9 %near_pack.1 = (f32[2,216,128]{2,1,0:T(8,128)S(1)}, f32[2,216,128]{2,1,0:T(8,128)}, f32[2,216,128]{2,1,0:T(8,128)}, f32[2,216,128]{2,1,0:T(8,128)S(1)}, f32[2,21...) custom-call(s32[222]{0:T(256)S(1)} %concatenate.9.meta, ...), custom_call_target="tpu_custom_call" | custom-call | tf_op jit(solution)/shard_map/near_pack/pallas_call | solution.py:390
  5.4 2.6 %collective-permute-start.1 = (f32[2,216,128]{2,1,0:T(8,128)}, f32[2,216,128]{2,1,0:T(8,128)S(1)}, u32[]{:S(2)}, u32[]{:S(2)}) collective-permute-start(f32[2,216,128]{2,1,0:T(8,128)} %get-tuple-element.58), channel_id=1, source_target_pairs={{0,2},{1,3},{2,0},{3,1},{4,6},{5,7},{6,4},{7,5},{8,10},{9,11},{10,... | collective-permute-start | bytes 663560 | tf_op jit(solution)/shard_map/ppermute | solution.py:406
  9.8 6.0 %all-to-all-start = ((s32[8,1,18]{2,1,0:T(1,128)}), s32[8,1,18]{2,1,0:T(1,128)S(1)}, u32[]{:S(2)}, u32[]{:S(2)}) async-start(s32[8,1,18]{2,1,0:T(1,128)} %bitcast.10), calls=%async_computation | async-start | bytes 8192 | tf_op jit(solution)/shard_map/all_to_all | solution.py:384
  16.8 5.6 %all-to-all-done = s32[8,1,18]{2,1,0:T(1,128)S(1)} async-done(((s32[8,1,18]{2,1,0:T(1,128)}), s32[8,1,18]{2,1,0:T(1,128)S(1)}, u32[]{:S(2)}, u32[]{:S(2)}) %all-to-all-start) | async-done | bytes 608 | tf_op jit(solution)/shard_map/all_to_all | solution.py:384
  22.3 2.4 %far_pack.1 = (f32[2,216,128]{2,1,0:T(8,128)S(1)}, f32[2,216,128]{2,1,0:T(8,128)S(1)}, f32[2,216,128]{2,1,0:T(8,128)S(1)}, f32[2,216,128]{2,1,0:T(8,128)S(1)}, f...) custom-call(s32[8,18]{1,0:T(8,128)S(1)} %bitcast.33, ...), custom_call_target="tpu_custom_call" | custom-call | tf_op jit(solution)/shard_map/far_pack/pallas_call | solution.py:407
  26.7 3.0 %collective-permute-start.19 = (f32[2,216,128]{2,1,0:T(8,128)S(1)}, f32[2,216,128]{2,1,0:T(8,128)S(1)}, u32[]{:S(2)}, u32[]{:S(2)}) collective-permute-start(f32[2,216,128]{2,1,0:T(8,128)S(1)} %get-tuple-element.85), channel_id=1, source_target_pairs={{0,26},{1,31},{2,16},{3,21},{4,30},{5,27},{6,20},{7,17},{8,18},{9,... | collective-permute-start | bytes 663560 | tf_op jit(solution)/shard_map/ppermute | solution.py:427
  29.7 2.1 %collective-permute-start.20 = (f32[2,216,128]{2,1,0:T(8,128)S(1)}, f32[2,216,128]{2,1,0:T(8,128)S(1)}, u32[]{:S(2)}, u32[]{:S(2)}) collective-permute-start(f32[2,216,128]{2,1,0:T(8,128)S(1)} %get-tuple-element.86), channel_id=1, source_target_pairs={{0,31},{1,26},{2,21},{3,16},{4,27},{5,30},{6,17},{7,20},{8,23},{9,... | collective-permute-start | bytes 663560 | tf_op jit(solution)/shard_map/ppermute | solution.py:427
  32.9 18.6 %collective-permute-done.17.refs_4_ = f32[2,216,128]{2,1,0:T(8,128)S(1)} collective-permute-done((f32[2,216,128]{2,1,0:T(8,128)S(1)}, f32[2,216,128]{2,1,0:T(8,128)S(1)}, u32[]{:S(2)}, u32[]{:S(2)}) %collective-permute-start.17) | collective-permute-done | bytes 221216 | tf_op jit(solution)/shard_map/ppermute | solution.py:427
  52.2 3.3 %collective-permute-done.18.refs_5_ = f32[2,216,128]{2,1,0:T(8,128)S(1)} collective-permute-done((f32[2,216,128]{2,1,0:T(8,128)S(1)}, f32[2,216,128]{2,1,0:T(8,128)S(1)}, u32[]{:S(2)}, u32[]{:S(2)}) %collective-permute-start.18) | collective-permute-done | bytes 221216 | tf_op jit(solution)/shard_map/ppermute | solution.py:427
  55.5 1.6 %collective-permute-start.4 = (f32[2,216,128]{2,1,0:T(8,128)S(1)}, f32[2,216,128]{2,1,0:T(8,128)S(1)}, u32[]{:S(2)}, u32[]{:S(2)}) collective-permute-start(f32[2,216,128]{2,1,0:T(8,128)S(1)} %get-tuple-element.61), channel_id=1, source_target_pairs={{0,5},{1,0},{2,15},{3,10},{4,1},{5,4},{6,11},{7,14},{8,13},{9,8},{... | collective-permute-start | bytes 663560 | tf_op jit(solution)/shard_map/ppermute | solution.py:427
  57.1 5.4 %collective-permute-done.19.refs_6_ = f32[2,216,128]{2,1,0:T(8,128)S(1)} collective-permute-done((f32[2,216,128]{2,1,0:T(8,128)S(1)}, f32[2,216,128]{2,1,0:T(8,128)S(1)}, u32[]{:S(2)}, u32[]{:S(2)}) %collective-permute-start.19) | collective-permute-done | bytes 221216 | tf_op jit(solution)/shard_map/ppermute | solution.py:427
  62.8 1.6 %collective-permute-done.20.refs_7_ = f32[2,216,128]{2,1,0:T(8,128)S(1)} collective-permute-done((f32[2,216,128]{2,1,0:T(8,128)S(1)}, f32[2,216,128]{2,1,0:T(8,128)S(1)}, u32[]{:S(2)}, u32[]{:S(2)}) %collective-permute-start.20) | collective-permute-done | bytes 221216 | tf_op jit(solution)/shard_map/ppermute | solution.py:427
  64.4 3.8 %collective-permute-start.6 = (f32[2,216,128]{2,1,0:T(8,128)S(1)}, f32[2,216,128]{2,1,0:T(8,128)S(1)}, u32[]{:S(2)}, u32[]{:S(2)}) collective-permute-start(f32[2,216,128]{2,1,0:T(8,128)S(1)} %get-tuple-element.63), channel_id=1, source_target_pairs={{0,15},{1,10},{2,5},{3,0},{4,11},{5,14},{6,1},{7,4},{8,7},{9,2},{1... | collective-permute-start | bytes 663560 | tf_op jit(solution)/shard_map/ppermute | solution.py:427
  68.2 3.7 %shard_map.129 = (f32[2,216,128]{2,1,0:T(8,128)S(1)}, f32[2,216,128]{2,1,0:T(8,128)S(1)}, f32[2,216,128]{2,1,0:T(8,128)S(1)}, f32[2,216,128]{2,1,0:T(8,128)S(1)}...) custom-call(s32[6,16]{1,0:T(8,128)S(1)} %get-tuple-element.54.tab.ne, ...), custom_call_target="tpu_custom_call" | custom-call | flops 2000000000 | bytes 8000000 | tf_op jit(solution)/shard_map/pallas_call | solution.py:233
  72.7 1.9 %collective-permute-start.29 = (f32[1,216,128]{2,1,0:T(8,128)S(1)}, f32[1,216,128]{2,1,0:T(8,128)S(1)}, u32[]{:S(2)}, u32[]{:S(2)}) collective-permute-start(f32[1,216,128]{2,1,0:T(8,128)S(1)} %get-tuple-element.100), channel_id=1, source_target_pairs={{21,0},{16,1},{31,2},{26,3},{17,4},{20,5},{27,6},{30,7},{29,8},{24... | collective-permute-start | bytes 331784 | tf_op jit(solution)/shard_map/ppermute | solution.py:440
  75.4 3.9 %shard_map.127 = (f32[2,216,128]{2,1,0:T(8,128)S(1)}, f32[2,216,128]{2,1,0:T(8,128)S(1)}, f32[2,216,128]{2,1,0:T(8,128)S(1)}, f32[2,216,128]{2,1,0:T(8,128)S(1)}...) custom-call(s32[6,16]{1,0:T(8,128)S(1)} %get-tuple-element.54.tab.ne, ...), custom_call_target="tpu_custom_call" | custom-call | flops 2000000000 | bytes 8000000 | tf_op jit(solution)/shard_map/pallas_call | solution.py:233
  79.6 6.0 %collective-permute-start.8 = (f32[2,216,128]{2,1,0:T(8,128)S(1)}, f32[2,216,128]{2,1,0:T(8,128)S(1)}, u32[]{:S(2)}, u32[]{:S(2)}) collective-permute-start(f32[2,216,128]{2,1,0:T(8,128)S(1)} %get-tuple-element.73), channel_id=1, source_target_pairs={{0,2},{1,3},{2,0},{3,1},{4,6},{5,7},{6,4},{7,5},{8,10},{9,11},{10,... | collective-permute-start | bytes 663560 | tf_op jit(solution)/shard_map/ppermute | solution.py:442
  86.1 1.6 %collective-permute-start.24 = (f32[1,216,128]{2,1,0:T(8,128)S(1)}, f32[1,216,128]{2,1,0:T(8,128)S(1)}, u32[]{:S(2)}, u32[]{:S(2)}) collective-permute-start(f32[1,216,128]{2,1,0:T(8,128)S(1)} %get-tuple-element.95), channel_id=1, source_target_pairs={{16,0},{21,1},{26,2},{31,3},{20,4},{17,5},{30,6},{27,7},{24,8},{29... | collective-permute-start | bytes 331784 | tf_op jit(solution)/shard_map/ppermute | solution.py:440
  87.8 3.2 %collective-permute-start.25 = (f32[1,216,128]{2,1,0:T(8,128)S(1)}, f32[1,216,128]{2,1,0:T(8,128)S(1)}, u32[]{:S(2)}, u32[]{:S(2)}) collective-permute-start(f32[1,216,128]{2,1,0:T(8,128)S(1)} %get-tuple-element.96), channel_id=1, source_target_pairs={{21,0},{16,1},{31,2},{26,3},{17,4},{20,5},{27,6},{30,7},{29,8},{24... | collective-permute-start | bytes 331784 | tf_op jit(solution)/shard_map/ppermute | solution.py:440
  90.9 2.8 %collective-permute-done.31.refs_11_ = f32[1,216,128]{2,1,0:T(8,128)S(1)} collective-permute-done((f32[1,216,128]{2,1,0:T(8,128)S(1)}, f32[1,216,128]{2,1,0:T(8,128)S(1)}, u32[]{:S(2)}, u32[]{:S(2)}) %collective-permute-start.31) | collective-permute-done | bytes 110624 | tf_op jit(solution)/shard_map/ppermute | solution.py:440
  93.8 6.0 %collective-permute-done.24.refs_4_ = f32[1,216,128]{2,1,0:T(8,128)S(1)} collective-permute-done((f32[1,216,128]{2,1,0:T(8,128)S(1)}, f32[1,216,128]{2,1,0:T(8,128)S(1)}, u32[]{:S(2)}, u32[]{:S(2)}) %collective-permute-start.24) | collective-permute-done | bytes 110624 | tf_op jit(solution)/shard_map/ppermute | solution.py:440
  100.5 2.6 %collective-permute-done.25.refs_5_ = f32[1,216,128]{2,1,0:T(8,128)S(1)} collective-permute-done((f32[1,216,128]{2,1,0:T(8,128)S(1)}, f32[1,216,128]{2,1,0:T(8,128)S(1)}, u32[]{:S(2)}, u32[]{:S(2)}) %collective-permute-start.25) | collective-permute-done | bytes 110624 | tf_op jit(solution)/shard_map/ppermute | solution.py:440
  103.1 2.3 %collective-permute-start.11 = (f32[2,216,128]{2,1,0:T(8,128)S(1)}, f32[2,216,128]{2,1,0:T(8,128)S(1)}, u32[]{:S(2)}, u32[]{:S(2)}) collective-permute-start(f32[2,216,128]{2,1,0:T(8,128)S(1)} %get-tuple-element.76), channel_id=1, source_target_pairs={{5,0},{0,1},{15,2},{10,3},{1,4},{4,5},{11,6},{14,7},{13,8},{8,9},{... | collective-permute-start | bytes 663560 | tf_op jit(solution)/shard_map/ppermute | solution.py:440
  106.5 3.1 %collective-permute-start.22 = (f32[2,216,128]{2,1,0:T(8,128)S(1)}, f32[2,216,128]{2,1,0:T(8,128)S(1)}, u32[]{:S(2)}, u32[]{:S(2)}) collective-permute-start(f32[2,216,128]{2,1,0:T(8,128)S(1)} %get-tuple-element.93), channel_id=1, source_target_pairs={{0,2},{1,3},{2,0},{3,1},{4,6},{5,7},{6,4},{7,5},{8,10},{9,11},{10,... | collective-permute-start | bytes 663560 | tf_op jit(solution)/shard_map/ppermute | solution.py:442
  112.6 4.9 %collective-permute-done.12.refs_7_ = f32[2,216,128]{2,1,0:T(8,128)S(1)} collective-permute-done((f32[2,216,128]{2,1,0:T(8,128)S(1)}, f32[2,216,128]{2,1,0:T(8,128)S(1)}, u32[]{:S(2)}, u32[]{:S(2)}) %collective-permute-start.12) | collective-permute-done | bytes 221216 | tf_op jit(solution)/shard_map/ppermute | solution.py:440
  117.5 2.8 %collective-permute-start.26 = (f32[1,216,128]{2,1,0:T(8,128)S(1)}, f32[1,216,128]{2,1,0:T(8,128)S(1)}, u32[]{:S(2)}, u32[]{:S(2)}) collective-permute-start(f32[1,216,128]{2,1,0:T(8,128)S(1)} %get-tuple-element.97), channel_id=1, source_target_pairs={{26,0},{31,1},{16,2},{21,3},{30,4},{27,5},{20,6},{17,7},{18,8},{23... | collective-permute-start | bytes 331784 | tf_op jit(solution)/shard_map/ppermute | solution.py:440
  121.1 1.7 %collective-permute-start.27 = (f32[1,216,128]{2,1,0:T(8,128)S(1)}, f32[1,216,128]{2,1,0:T(8,128)S(1)}, u32[]{:S(2)}, u32[]{:S(2)}) collective-permute-start(f32[1,216,128]{2,1,0:T(8,128)S(1)} %get-tuple-element.98), channel_id=1, source_target_pairs={{31,0},{26,1},{21,2},{16,3},{27,4},{30,5},{17,6},{20,7},{23,8},{18... | collective-permute-start | bytes 331784 | tf_op jit(solution)/shard_map/ppermute | solution.py:440
  122.8 2.0 %shard_map.128.base = f32[1728,128]{1,0:T(8,128)} custom-call(s32[6,16]{1,0:T(8,128)S(1)} %get-tuple-element.54.tab.near_tab, s32[2,16]{1,0:T(2,128)S(1)} %get-tuple-element.55.far_tab, f32[1728,128]{1,0:T(8,128)S(1)} %bitcast.32, f32[1728,128]{1,0:T(8,128)S(1)} %bitcast.31, f32[2,216,128]{2,1,0:T(8,128)S(1)} %get-tuple-element.71.refs_1_, ...), custom_call_target="tpu_custom_call" | custom-call | tf_op jit(solution)/shard_map/pallas_call | solution.py:450
  124.8 3.0 %collective-permute-done.26.refs_6_ = f32[1,216,128]{2,1,0:T(8,128)S(1)} collective-permute-done((f32[1,216,128]{2,1,0:T(8,128)S(1)}, f32[1,216,128]{2,1,0:T(8,128)S(1)}, u32[]{:S(2)}, u32[]{:S(2)}) %collective-permute-start.26) | collective-permute-done | bytes 110624 | tf_op jit(solution)/shard_map/ppermute | solution.py:440
  127.8 2.4 %collective-permute-done.27.refs_7_ = f32[1,216,128]{2,1,0:T(8,128)S(1)} collective-permute-done((f32[1,216,128]{2,1,0:T(8,128)S(1)}, f32[1,216,128]{2,1,0:T(8,128)S(1)}, u32[]{:S(2)}, u32[]{:S(2)}) %collective-permute-start.27) | collective-permute-done | bytes 110624 | tf_op jit(solution)/shard_map/ppermute | solution.py:440
  130.2 4.6 %collective-permute-done.23.refs_3_ = f32[2,216,128]{2,1,0:T(8,128)S(1)} collective-permute-done((f32[2,216,128]{2,1,0:T(8,128)S(1)}, f32[2,216,128]{2,1,0:T(8,128)S(1)}, u32[]{:S(2)}, u32[]{:S(2)}) %collective-permute-start.23) | collective-permute-done | bytes 221216 | tf_op jit(solution)/shard_map/ppermute | solution.py:442
  134.8 2.5 %shard_map.131 = f32[1728,128]{1,0:T(8,128)} custom-call(s32[6,16]{1,0:T(8,128)S(1)} %get-tuple-element.54.tab.near_tab, s32[2,16]{1,0:T(2,128)S(1)} %get-tuple-element.55.far_tab, f32[1728,128]{1,0:T(8,128)} %shard_map.128.base, f32[2,216,128]{2,1,0:T(8,128)S(1)} %get-tuple-element.91.refs_0_, ...), custom_call_target="tpu_custom_call", output_to_operand_aliasing={{}: (2, {})} | custom-call | tf_op jit(solution)/shard_map/pallas_call | solution.py:450
  (64 shorter events, 18.1 us)
Async XLA Ops:
  4.8 20.0 %collective-permute-start = (f32[2,216,128]{2,1,0:T(8,128)}, f32[2,216,128]{2,1,0:T(8,128)S(1)}, u32[]{:S(2)}, u32[]{:S(2)}) collective-permute-start(f32[2,216,128]{2,1,0:T(8,128)} %get-tuple-element.57), channel_id=1, source_target_pairs={{0,1},{1,0},{2,3},{3,2},{4,5},{5,4},{6,7},{7,6},{8,9},{9,8},{10,11... | collective-permute-start | bytes 663560 | tf_op jit(solution)/shard_map/ppermute | solution.py:406
  5.4 19.9 %collective-permute-start.1 = (f32[2,216,128]{2,1,0:T(8,128)}, f32[2,216,128]{2,1,0:T(8,128)S(1)}, u32[]{:S(2)}, u32[]{:S(2)}) collective-permute-start(f32[2,216,128]{2,1,0:T(8,128)} %get-tuple-element.58), channel_id=1, source_target_pairs={{0,2},{1,3},{2,0},{3,1},{4,6},{5,7},{6,4},{7,5},{8,10},{9,11},{10,... | collective-permute-start | bytes 663560 | tf_op jit(solution)/shard_map/ppermute | solution.py:406
  8.0 18.7 %collective-permute-start.14 = (f32[2,216,128]{2,1,0:T(8,128)S(1)}, f32[2,216,128]{2,1,0:T(8,128)S(1)}, u32[]{:S(2)}, u32[]{:S(2)}) collective-permute-start(f32[2,216,128]{2,1,0:T(8,128)S(1)} %get-tuple-element.80), channel_id=1, source_target_pairs={{0,1},{1,0},{2,3},{3,2},{4,5},{5,4},{6,7},{7,6},{8,9},{9,8},{10,11... | collective-permute-start | bytes 663560 | tf_op jit(solution)/shard_map/ppermute | solution.py:406
  8.1 21.6 %collective-permute-start.15 = (f32[2,216,128]{2,1,0:T(8,128)S(1)}, f32[2,216,128]{2,1,0:T(8,128)S(1)}, u32[]{:S(2)}, u32[]{:S(2)}) collective-permute-start(f32[2,216,128]{2,1,0:T(8,128)S(1)} %get-tuple-element.81), channel_id=1, source_target_pairs={{0,2},{1,3},{2,0},{3,1},{4,6},{5,7},{6,4},{7,5},{8,10},{9,11},{10,... | collective-permute-start | bytes 663560 | tf_op jit(solution)/shard_map/ppermute | solution.py:406
  9.8 12.5 %all-to-all-start = ((s32[8,1,18]{2,1,0:T(1,128)}), s32[8,1,18]{2,1,0:T(1,128)S(1)}, u32[]{:S(2)}, u32[]{:S(2)}) async-start(s32[8,1,18]{2,1,0:T(1,128)} %bitcast.10), calls=%async_computation | async-start | bytes 8192 | tf_op jit(solution)/shard_map/all_to_all | solution.py:384
  15.9 16.9 %collective-permute-start.16 = (f32[2,216,128]{2,1,0:T(8,128)S(1)}, f32[2,216,128]{2,1,0:T(8,128)S(1)}, u32[]{:S(2)}, u32[]{:S(2)}) collective-permute-start(f32[2,216,128]{2,1,0:T(8,128)S(1)} %get-tuple-element.82), channel_id=1, source_target_pairs={{0,3},{1,2},{2,1},{3,0},{4,7},{5,6},{6,5},{7,4},{8,11},{9,10},{10,... | collective-permute-start | bytes 663560 | tf_op jit(solution)/shard_map/ppermute | solution.py:406
  24.8 26.7 %collective-permute-start.17 = (f32[2,216,128]{2,1,0:T(8,128)S(1)}, f32[2,216,128]{2,1,0:T(8,128)S(1)}, u32[]{:S(2)}, u32[]{:S(2)}) collective-permute-start(f32[2,216,128]{2,1,0:T(8,128)S(1)} %get-tuple-element.83), channel_id=1, source_target_pairs={{0,16},{1,21},{2,26},{3,31},{4,20},{5,17},{6,30},{7,27},{8,24},{9,... | collective-permute-start | bytes 663560 | tf_op jit(solution)/shard_map/ppermute | solution.py:427
  25.3 30.1 %collective-permute-start.18 = (f32[2,216,128]{2,1,0:T(8,128)S(1)}, f32[2,216,128]{2,1,0:T(8,128)S(1)}, u32[]{:S(2)}, u32[]{:S(2)}) collective-permute-start(f32[2,216,128]{2,1,0:T(8,128)S(1)} %get-tuple-element.84), channel_id=1, source_target_pairs={{0,21},{1,16},{2,31},{3,26},{4,17},{5,20},{6,27},{7,30},{8,29},{9,... | collective-permute-start | bytes 663560 | tf_op jit(solution)/shard_map/ppermute | solution.py:427
  26.7 35.8 %collective-permute-start.19 = (f32[2,216,128]{2,1,0:T(8,128)S(1)}, f32[2,216,128]{2,1,0:T(8,128)S(1)}, u32[]{:S(2)}, u32[]{:S(2)}) collective-permute-start(f32[2,216,128]{2,1,0:T(8,128)S(1)} %get-tuple-element.85), channel_id=1, source_target_pairs={{0,26},{1,31},{2,16},{3,21},{4,30},{5,27},{6,20},{7,17},{8,18},{9,... | collective-permute-start | bytes 663560 | tf_op jit(solution)/shard_map/ppermute | solution.py:427
  29.7 34.7 %collective-permute-start.20 = (f32[2,216,128]{2,1,0:T(8,128)S(1)}, f32[2,216,128]{2,1,0:T(8,128)S(1)}, u32[]{:S(2)}, u32[]{:S(2)}) collective-permute-start(f32[2,216,128]{2,1,0:T(8,128)S(1)} %get-tuple-element.86), channel_id=1, source_target_pairs={{0,31},{1,26},{2,21},{3,16},{4,27},{5,30},{6,17},{7,20},{8,23},{9,... | collective-permute-start | bytes 663560 | tf_op jit(solution)/shard_map/ppermute | solution.py:427
  32.8 39.8 %collective-permute-start.2 = (f32[2,216,128]{2,1,0:T(8,128)S(1)}, f32[2,216,128]{2,1,0:T(8,128)S(1)}, u32[]{:S(2)}, u32[]{:S(2)}) collective-permute-start(f32[2,216,128]{2,1,0:T(8,128)S(1)} %get-tuple-element.59), channel_id=1, source_target_pairs={{0,3},{1,2},{2,1},{3,0},{4,7},{5,6},{6,5},{7,4},{8,11},{9,10},{10,... | collective-permute-start | bytes 663560 | tf_op jit(solution)/shard_map/ppermute | solution.py:406
  51.5 21.2 %collective-permute-start.3 = (f32[2,216,128]{2,1,0:T(8,128)S(1)}, f32[2,216,128]{2,1,0:T(8,128)S(1)}, u32[]{:S(2)}, u32[]{:S(2)}) collective-permute-start(f32[2,216,128]{2,1,0:T(8,128)S(1)} %get-tuple-element.60), channel_id=1, source_target_pairs={{0,0},{1,5},{2,10},{3,15},{4,4},{5,1},{6,14},{7,11},{8,8},{9,13},{... | collective-permute-start | bytes 663560 | tf_op jit(solution)/shard_map/ppermute | solution.py:427
  55.5 19.1 %collective-permute-start.4 = (f32[2,216,128]{2,1,0:T(8,128)S(1)}, f32[2,216,128]{2,1,0:T(8,128)S(1)}, u32[]{:S(2)}, u32[]{:S(2)}) collective-permute-start(f32[2,216,128]{2,1,0:T(8,128)S(1)} %get-tuple-element.61), channel_id=1, source_target_pairs={{0,5},{1,0},{2,15},{3,10},{4,1},{5,4},{6,11},{7,14},{8,13},{9,8},{... | collective-permute-start | bytes 663560 | tf_op jit(solution)/shard_map/ppermute | solution.py:427
  62.5 12.8 %collective-permute-start.5 = (f32[2,216,128]{2,1,0:T(8,128)S(1)}, f32[2,216,128]{2,1,0:T(8,128)S(1)}, u32[]{:S(2)}, u32[]{:S(2)}) collective-permute-start(f32[2,216,128]{2,1,0:T(8,128)S(1)} %get-tuple-element.62), channel_id=1, source_target_pairs={{0,10},{1,15},{2,0},{3,5},{4,14},{5,11},{6,4},{7,1},{8,2},{9,7},{1... | collective-permute-start | bytes 663560 | tf_op jit(solution)/shard_map/ppermute | solution.py:427
  64.4 10.9 %collective-permute-start.6 = (f32[2,216,128]{2,1,0:T(8,128)S(1)}, f32[2,216,128]{2,1,0:T(8,128)S(1)}, u32[]{:S(2)}, u32[]{:S(2)}) collective-permute-start(f32[2,216,128]{2,1,0:T(8,128)S(1)} %get-tuple-element.63), channel_id=1, source_target_pairs={{0,15},{1,10},{2,5},{3,0},{4,11},{5,14},{6,1},{7,4},{8,7},{9,2},{1... | collective-permute-start | bytes 663560 | tf_op jit(solution)/shard_map/ppermute | solution.py:427
  72.6 13.0 %collective-permute-start.28 = (f32[1,216,128]{2,1,0:T(8,128)S(1)}, f32[1,216,128]{2,1,0:T(8,128)S(1)}, u32[]{:S(2)}, u32[]{:S(2)}) collective-permute-start(f32[1,216,128]{2,1,0:T(8,128)S(1)} %get-tuple-element.99), channel_id=1, source_target_pairs={{16,0},{21,1},{26,2},{31,3},{20,4},{17,5},{30,6},{27,7},{24,8},{29... | collective-permute-start | bytes 331784 | tf_op jit(solution)/shard_map/ppermute | solution.py:440
  72.7 13.4 %collective-permute-start.29 = (f32[1,216,128]{2,1,0:T(8,128)S(1)}, f32[1,216,128]{2,1,0:T(8,128)S(1)}, u32[]{:S(2)}, u32[]{:S(2)}) collective-permute-start(f32[1,216,128]{2,1,0:T(8,128)S(1)} %get-tuple-element.100), channel_id=1, source_target_pairs={{21,0},{16,1},{31,2},{26,3},{17,4},{20,5},{27,6},{30,7},{29,8},{24... | collective-permute-start | bytes 331784 | tf_op jit(solution)/shard_map/ppermute | solution.py:440
  74.6 13.2 %collective-permute-start.30 = (f32[1,216,128]{2,1,0:T(8,128)S(1)}, f32[1,216,128]{2,1,0:T(8,128)S(1)}, u32[]{:S(2)}, u32[]{:S(2)}) collective-permute-start(f32[1,216,128]{2,1,0:T(8,128)S(1)} %get-tuple-element.101), channel_id=1, source_target_pairs={{26,0},{31,1},{16,2},{21,3},{30,4},{27,5},{20,6},{17,7},{18,8},{23... | collective-permute-start | bytes 331784 | tf_op jit(solution)/shard_map/ppermute | solution.py:440
  79.3 26.1 %collective-permute-start.7 = (f32[2,216,128]{2,1,0:T(8,128)S(1)}, f32[2,216,128]{2,1,0:T(8,128)S(1)}, u32[]{:S(2)}, u32[]{:S(2)}) collective-permute-start(f32[2,216,128]{2,1,0:T(8,128)S(1)} %get-tuple-element.72), channel_id=1, source_target_pairs={{0,1},{1,0},{2,3},{3,2},{4,5},{5,4},{6,7},{7,6},{8,9},{9,8},{10,11... | collective-permute-start | bytes 663560 | tf_op jit(solution)/shard_map/ppermute | solution.py:442
  79.6 26.1 %collective-permute-start.8 = (f32[2,216,128]{2,1,0:T(8,128)S(1)}, f32[2,216,128]{2,1,0:T(8,128)S(1)}, u32[]{:S(2)}, u32[]{:S(2)}) collective-permute-start(f32[2,216,128]{2,1,0:T(8,128)S(1)} %get-tuple-element.73), channel_id=1, source_target_pairs={{0,2},{1,3},{2,0},{3,1},{4,6},{5,7},{6,4},{7,5},{8,10},{9,11},{10,... | collective-permute-start | bytes 663560 | tf_op jit(solution)/shard_map/ppermute | solution.py:442
  85.6 8.1 %collective-permute-start.31 = (f32[1,216,128]{2,1,0:T(8,128)S(1)}, f32[1,216,128]{2,1,0:T(8,128)S(1)}, u32[]{:S(2)}, u32[]{:S(2)}) collective-permute-start(f32[1,216,128]{2,1,0:T(8,128)S(1)} %get-tuple-element.102), channel_id=1, source_target_pairs={{31,0},{26,1},{21,2},{16,3},{27,4},{30,5},{17,6},{20,7},{23,8},{18... | collective-permute-start | bytes 331784 | tf_op jit(solution)/shard_map/ppermute | solution.py:440
  86.1 13.7 %collective-permute-start.24 = (f32[1,216,128]{2,1,0:T(8,128)S(1)}, f32[1,216,128]{2,1,0:T(8,128)S(1)}, u32[]{:S(2)}, u32[]{:S(2)}) collective-permute-start(f32[1,216,128]{2,1,0:T(8,128)S(1)} %get-tuple-element.95), channel_id=1, source_target_pairs={{16,0},{21,1},{26,2},{31,3},{20,4},{17,5},{30,6},{27,7},{24,8},{29... | collective-permute-start | bytes 331784 | tf_op jit(solution)/shard_map/ppermute | solution.py:440
  87.8 15.3 %collective-permute-start.25 = (f32[1,216,128]{2,1,0:T(8,128)S(1)}, f32[1,216,128]{2,1,0:T(8,128)S(1)}, u32[]{:S(2)}, u32[]{:S(2)}) collective-permute-start(f32[1,216,128]{2,1,0:T(8,128)S(1)} %get-tuple-element.96), channel_id=1, source_target_pairs={{21,0},{16,1},{31,2},{26,3},{17,4},{20,5},{27,6},{30,7},{29,8},{24... | collective-permute-start | bytes 331784 | tf_op jit(solution)/shard_map/ppermute | solution.py:440
  93.8 12.7 %collective-permute-start.9 = (f32[2,216,128]{2,1,0:T(8,128)S(1)}, f32[2,216,128]{2,1,0:T(8,128)S(1)}, u32[]{:S(2)}, u32[]{:S(2)}) collective-permute-start(f32[2,216,128]{2,1,0:T(8,128)S(1)} %get-tuple-element.74), channel_id=1, source_target_pairs={{0,3},{1,2},{2,1},{3,0},{4,7},{5,6},{6,5},{7,4},{8,11},{9,10},{10,... | collective-permute-start | bytes 663560 | tf_op jit(solution)/shard_map/ppermute | solution.py:442
  103.1 8.1 %collective-permute-start.11 = (f32[2,216,128]{2,1,0:T(8,128)S(1)}, f32[2,216,128]{2,1,0:T(8,128)S(1)}, u32[]{:S(2)}, u32[]{:S(2)}) collective-permute-start(f32[2,216,128]{2,1,0:T(8,128)S(1)} %get-tuple-element.76), channel_id=1, source_target_pairs={{5,0},{0,1},{15,2},{10,3},{1,4},{4,5},{11,6},{14,7},{13,8},{8,9},{... | collective-permute-start | bytes 663560 | tf_op jit(solution)/shard_map/ppermute | solution.py:440
  105.4 12.1 %collective-permute-start.12 = (f32[2,216,128]{2,1,0:T(8,128)S(1)}, f32[2,216,128]{2,1,0:T(8,128)S(1)}, u32[]{:S(2)}, u32[]{:S(2)}) collective-permute-start(f32[2,216,128]{2,1,0:T(8,128)S(1)} %get-tuple-element.77), channel_id=1, source_target_pairs={{10,0},{15,1},{0,2},{5,3},{14,4},{11,5},{4,6},{1,7},{2,8},{7,9},{8... | collective-permute-start | bytes 663560 | tf_op jit(solution)/shard_map/ppermute | solution.py:440
  105.7 15.4 %collective-permute-start.13 = (f32[2,216,128]{2,1,0:T(8,128)S(1)}, f32[2,216,128]{2,1,0:T(8,128)S(1)}, u32[]{:S(2)}, u32[]{:S(2)}) collective-permute-start(f32[2,216,128]{2,1,0:T(8,128)S(1)} %get-tuple-element.78), channel_id=1, source_target_pairs={{15,0},{10,1},{5,2},{0,3},{11,4},{14,5},{1,6},{4,7},{7,8},{2,9},{1... | collective-permute-start | bytes 663560 | tf_op jit(solution)/shard_map/ppermute | solution.py:440
  106.4 23.8 %collective-permute-start.21 = (f32[2,216,128]{2,1,0:T(8,128)S(1)}, f32[2,216,128]{2,1,0:T(8,128)S(1)}, u32[]{:S(2)}, u32[]{:S(2)}) collective-permute-start(f32[2,216,128]{2,1,0:T(8,128)S(1)} %get-tuple-element.92), channel_id=1, source_target_pairs={{0,1},{1,0},{2,3},{3,2},{4,5},{5,4},{6,7},{7,6},{8,9},{9,8},{10,11... | collective-permute-start | bytes 663560 | tf_op jit(solution)/shard_map/ppermute | solution.py:442
  106.5 23.7 %collective-permute-start.22 = (f32[2,216,128]{2,1,0:T(8,128)S(1)}, f32[2,216,128]{2,1,0:T(8,128)S(1)}, u32[]{:S(2)}, u32[]{:S(2)}) collective-permute-start(f32[2,216,128]{2,1,0:T(8,128)S(1)} %get-tuple-element.93), channel_id=1, source_target_pairs={{0,2},{1,3},{2,0},{3,1},{4,6},{5,7},{6,4},{7,5},{8,10},{9,11},{10,... | collective-permute-start | bytes 663560 | tf_op jit(solution)/shard_map/ppermute | solution.py:442
  111.2 23.6 %collective-permute-start.23 = (f32[2,216,128]{2,1,0:T(8,128)S(1)}, f32[2,216,128]{2,1,0:T(8,128)S(1)}, u32[]{:S(2)}, u32[]{:S(2)}) collective-permute-start(f32[2,216,128]{2,1,0:T(8,128)S(1)} %get-tuple-element.94), channel_id=1, source_target_pairs={{0,3},{1,2},{2,1},{3,0},{4,7},{5,6},{6,5},{7,4},{8,11},{9,10},{10,... | collective-permute-start | bytes 663560 | tf_op jit(solution)/shard_map/ppermute | solution.py:442
  117.5 10.3 %collective-permute-start.26 = (f32[1,216,128]{2,1,0:T(8,128)S(1)}, f32[1,216,128]{2,1,0:T(8,128)S(1)}, u32[]{:S(2)}, u32[]{:S(2)}) collective-permute-start(f32[1,216,128]{2,1,0:T(8,128)S(1)} %get-tuple-element.97), channel_id=1, source_target_pairs={{26,0},{31,1},{16,2},{21,3},{30,4},{27,5},{20,6},{17,7},{18,8},{23... | collective-permute-start | bytes 331784 | tf_op jit(solution)/shard_map/ppermute | solution.py:440
  121.1 9.1 %collective-permute-start.27 = (f32[1,216,128]{2,1,0:T(8,128)S(1)}, f32[1,216,128]{2,1,0:T(8,128)S(1)}, u32[]{:S(2)}, u32[]{:S(2)}) collective-permute-start(f32[1,216,128]{2,1,0:T(8,128)S(1)} %get-tuple-element.98), channel_id=1, source_target_pairs={{31,0},{26,1},{21,2},{16,3},{27,4},{30,5},{17,6},{20,7},{23,8},{18... | collective-permute-start | bytes 331784 | tf_op jit(solution)/shard_map/ppermute | solution.py:440
  (8 other events, 232.6 us)

commit v2 on v1

--- a/solution.py
+++ b/solution.py
@@ -377,10 +377,9 @@
     meta = jnp.concatenate(
         [gid[None], sid[None], owner, pair_remote[0], pair_resident[0], pair_count[0], offsets.reshape(-1)]
     )
-    where = lax.broadcasted_iota(jnp.int32, (groups, 2), 0)
-    where = jnp.where(lax.broadcasted_iota(jnp.int32, (groups, 2), 1) == 0, where, sid)
-    mine = jnp.concatenate([owner, pair_remote[0]])
-    mine = jnp.concatenate([jnp.broadcast_to(mine[None], (groups, 2 * listed)), where], axis=1)
+    line = jnp.concatenate([owner, pair_remote[0], sid[None], sid[None]])[None]
+    place = lax.broadcasted_iota(jnp.int32, (groups, 2 * listed + 2), 1)
+    mine = jnp.where(place == 2 * listed, lax.broadcasted_iota(jnp.int32, place.shape, 0), line)
     lists = lax.all_to_all(mine, "grp", 0, 0, tiled=True)
     rows = as_rows(orbitals)
     pot_rows = as_rows(local_pot)
@@ -440,19 +439,21 @@
                 far_back[q, k, ranks] = lax.ppermute(far_out[k], ("grp", "slc"), back)
         for k in range(slices):
             near_back[q, k, every] = earlier[k] if k == 0 else lax.ppermute(earlier[k], "slc", across[k])
+    last = rounds - 1
+    steps = [([x for x in near_back if x[0] < last], [x for x in far_back if x[0] < last])]
+    for ranks in rank_sets(last, rounds):
+        steps.append(([x for x in near_back if x[0] == last and not ranks[0]], [x for x in far_back if x[::2] == (last, ranks)]))
     out = None
-    for chosen in (tuple(range(rounds - 1)), (rounds - 1,)):
+    for step, (near_keys, far_keys) in enumerate(steps):
         first = out is None
-        base = [pot_rows, rows] if first else [out]
-        near_keys = [x for x in near_back if x[0] in chosen]
-        far_keys = [x for x in far_back if x[0] in chosen]
+        ended = step == len(steps) - 1
+        base = [pot_rows, rows] if first else [kept(out)]
         parts = [kept(near_back[x]) for x in near_keys] + [kept(far_back[x]) for x in far_keys]
         out = pl.pallas_call(
             functools.partial(sum_kernel, slices, orbs, planes, near_keys, far_keys, first),
             in_specs=[smem()] * 2 + [vmem()] * (len(base) + len(parts)),
             out_specs=vmem(),
-            out_shape=jax.ShapeDtypeStruct(rows.shape, jnp.float32),
-            input_output_aliases={} if first else {2: 0},
+            out_shape=jax.ShapeDtypeStruct(rows.shape, jnp.float32) if ended else pltpu.VMEM(rows.shape, jnp.float32),
             compiler_params=grant(6),
         )(near_tab, far_tab, *base, *parts)
     out = out.reshape(planes, orbs // 8, cells // LANES, 8, LANES).transpose(0, 1, 3, 2, 4)

time: 138 us -> 134 us (0.971)
  starting transfers between devices: 50.1 us -> 46 us
    ppermute x12, waiting for transfers between devices: 24.7 us -> 12.6 us  [operator(): far_back[q, k, ranks] = lax.ppermute(far_out[k], ('grp', 'slc'), back)]
    ppermute x6, waiting for transfers between devices: 4.63 us -> 16.4 us  [operator(): lax.ppermute(earlier[k], 'slc', across[k])]
    ppermute x6, starting transfers between devices: 10.9 us -> 4.19 us  [operator(): lax.ppermute(earlier[k], 'slc', across[k])]
    ppermute x12, starting transfers between devices: 15.2 us -> 17.9 us  [operator(): far_back[q, k, ranks] = lax.ppermute(far_out[k], ('grp', 'slc'), back)]
    pallas_call x2 -> x3, Pallas kernels: 4.5 us -> 3.69 us  [operator(): pl.pallas_call(functools.partial(sum_kernel, slices, orbs, planes, near_k...]
  transfers between devices with their start and end apart: 33 -> 33, of which waited for: 17 -> 13; matrix products, arithmetic and copies ran while one was open for 1% -> 1% of each run, Pallas kernels for 10% -> 10%
where the time goes in v2:
time: 134 us; the launch traced here: 132 us
  waiting for transfers between devices  65 us (49%)
  starting transfers between devices  46 us (34%)
  Pallas kernels  16.9 us (13%)
  local copies, waits for them, and re-layouts  2.92 us (2%)
  other arithmetic  1.35 us (1%)
    ppermute x8, waiting for transfers between devices, operator(): lax.ppermute(sends[q * slices + k], ('grp', 'slc'), there(q, k))  30.4 us
    ppermute x12, starting transfers between devices, operator(): far_back[q, k, ranks] = lax.ppermute(far_out[k], ('grp', 'slc'), back)  17.9 us
    ppermute x6, waiting for transfers between devices, operator(): lax.ppermute(earlier[k], 'slc', across[k])  16.4 us
    ppermute x8, starting transfers between devices, operator(): lax.ppermute(sends[q * slices + k], ('grp', 'slc'), there(q, k))  13.3 us
    ppermute x12, waiting for transfers between devices, operator(): far_back[q, k, ranks] = lax.ppermute(far_out[k], ('grp', 'slc'), back)  12.6 us
    pallas_call x3, Pallas kernels, pair_call(): pl.pallas_call(functools.partial(pair_kernel, slices, slab, round_id, ran...  7.92 us
    all_to_all x1, starting transfers between devices, operator(): lists = lax.all_to_all(mine, 'grp', 0, 0, tiled=True)  6.03 us
    all_to_all x1, waiting for transfers between devices, operator(): lists = lax.all_to_all(mine, 'grp', 0, 0, tiled=True)  5.55 us
  transfers between devices with their start and end apart: 33, of which 13 were waited for; matrix products, arithmetic and copies ran while one was open for 1% of the time, Pallas kernels for 10%

profile of v2, /device:TPU:0, one launch (start us, length us, event | category | flops | bytes accessed | tf_op | source)
XLA Modules:
  0.0 132.4 jit_solution(1481091717182046294)
XLA Ops:
  1.7 1.2 copy-done
  2.9 1.9 %near_pack.1 = (f32[2,216,128]{2,1,0:T(8,128)S(1)}, f32[2,216,128]{2,1,0:T(8,128)}, f32[2,216,128]{2,1,0:T(8,128)}, f32[2,216,128]{2,1,0:T(8,128)S(1)}, f32[2,21...) custom-call(s32[222]{0:T(256)S(1)} %concatenate.6.meta, ...), custom_call_target="tpu_custom_call" | custom-call | tf_op jit(solution)/shard_map/near_pack/pallas_call | solution.py:389
  5.4 2.6 %collective-permute-start.1 = (f32[2,216,128]{2,1,0:T(8,128)}, f32[2,216,128]{2,1,0:T(8,128)S(1)}, u32[]{:S(2)}, u32[]{:S(2)}) collective-permute-start(f32[2,216,128]{2,1,0:T(8,128)} %get-tuple-element.58), channel_id=1, source_target_pairs={{0,2},{1,3},{2,0},{3,1},{4,6},{5,7},{6,4},{7,5},{8,10},{9,11},{10,... | collective-permute-start | bytes 663560 | tf_op jit(solution)/shard_map/ppermute | solution.py:405
  9.8 6.0 %all-to-all-start = ((s32[8,1,18]{2,1,0:T(1,128)}), s32[8,1,18]{2,1,0:T(1,128)S(1)}, u32[]{:S(2)}, u32[]{:S(2)}) async-start(s32[8,1,18]{2,1,0:T(1,128)} %broadcast_select_fusion), calls=%async_computation | async-start | bytes 8192 | tf_op jit(solution)/shard_map/all_to_all | solution.py:383
  16.7 5.6 %all-to-all-done = s32[8,1,18]{2,1,0:T(1,128)S(1)} async-done(((s32[8,1,18]{2,1,0:T(1,128)}), s32[8,1,18]{2,1,0:T(1,128)S(1)}, u32[]{:S(2)}, u32[]{:S(2)}) %all-to-all-start) | async-done | bytes 608 | tf_op jit(solution)/shard_map/all_to_all | solution.py:383
  22.3 2.4 %far_pack.1 = (f32[2,216,128]{2,1,0:T(8,128)S(1)}, f32[2,216,128]{2,1,0:T(8,128)S(1)}, f32[2,216,128]{2,1,0:T(8,128)S(1)}, f32[2,216,128]{2,1,0:T(8,128)S(1)}, f...) custom-call(s32[8,18]{1,0:T(8,128)S(1)} %bitcast.32, ...), custom_call_target="tpu_custom_call" | custom-call | tf_op jit(solution)/shard_map/far_pack/pallas_call | solution.py:406
  25.3 1.4 %collective-permute-start.18 = (f32[2,216,128]{2,1,0:T(8,128)S(1)}, f32[2,216,128]{2,1,0:T(8,128)S(1)}, u32[]{:S(2)}, u32[]{:S(2)}) collective-permute-start(f32[2,216,128]{2,1,0:T(8,128)S(1)} %get-tuple-element.84), channel_id=1, source_target_pairs={{0,21},{1,16},{2,31},{3,26},{4,17},{5,20},{6,27},{7,30},{8,29},{9,... | collective-permute-start | bytes 663560 | tf_op jit(solution)/shard_map/ppermute | solution.py:426
  26.6 3.0 %collective-permute-start.19 = (f32[2,216,128]{2,1,0:T(8,128)S(1)}, f32[2,216,128]{2,1,0:T(8,128)S(1)}, u32[]{:S(2)}, u32[]{:S(2)}) collective-permute-start(f32[2,216,128]{2,1,0:T(8,128)S(1)} %get-tuple-element.85), channel_id=1, source_target_pairs={{0,26},{1,31},{2,16},{3,21},{4,30},{5,27},{6,20},{7,17},{8,18},{9,... | collective-permute-start | bytes 663560 | tf_op jit(solution)/shard_map/ppermute | solution.py:426
  29.6 2.1 %collective-permute-start.20 = (f32[2,216,128]{2,1,0:T(8,128)S(1)}, f32[2,216,128]{2,1,0:T(8,128)S(1)}, u32[]{:S(2)}, u32[]{:S(2)}) collective-permute-start(f32[2,216,128]{2,1,0:T(8,128)S(1)} %get-tuple-element.86), channel_id=1, source_target_pairs={{0,31},{1,26},{2,21},{3,16},{4,27},{5,30},{6,17},{7,20},{8,23},{9,... | collective-permute-start | bytes 663560 | tf_op jit(solution)/shard_map/ppermute | solution.py:426
  31.7 19.7 %collective-permute-done.17.refs_4_ = f32[2,216,128]{2,1,0:T(8,128)S(1)} collective-permute-done((f32[2,216,128]{2,1,0:T(8,128)S(1)}, f32[2,216,128]{2,1,0:T(8,128)S(1)}, u32[]{:S(2)}, u32[]{:S(2)}) %collective-permute-start.17) | collective-permute-done | bytes 221216 | tf_op jit(solution)/shard_map/ppermute | solution.py:426
  52.1 3.3 %collective-permute-done.18.refs_5_ = f32[2,216,128]{2,1,0:T(8,128)S(1)} collective-permute-done((f32[2,216,128]{2,1,0:T(8,128)S(1)}, f32[2,216,128]{2,1,0:T(8,128)S(1)}, u32[]{:S(2)}, u32[]{:S(2)}) %collective-permute-start.18) | collective-permute-done | bytes 221216 | tf_op jit(solution)/shard_map/ppermute | solution.py:426
  55.4 1.6 %collective-permute-start.4 = (f32[2,216,128]{2,1,0:T(8,128)S(1)}, f32[2,216,128]{2,1,0:T(8,128)S(1)}, u32[]{:S(2)}, u32[]{:S(2)}) collective-permute-start(f32[2,216,128]{2,1,0:T(8,128)S(1)} %get-tuple-element.61), channel_id=1, source_target_pairs={{0,5},{1,0},{2,15},{3,10},{4,1},{5,4},{6,11},{7,14},{8,13},{9,8},{... | collective-permute-start | bytes 663560 | tf_op jit(solution)/shard_map/ppermute | solution.py:426
  57.0 5.4 %collective-permute-done.19.refs_6_ = f32[2,216,128]{2,1,0:T(8,128)S(1)} collective-permute-done((f32[2,216,128]{2,1,0:T(8,128)S(1)}, f32[2,216,128]{2,1,0:T(8,128)S(1)}, u32[]{:S(2)}, u32[]{:S(2)}) %collective-permute-start.19) | collective-permute-done | bytes 221216 | tf_op jit(solution)/shard_map/ppermute | solution.py:426
  62.7 1.6 %collective-permute-done.20.refs_7_ = f32[2,216,128]{2,1,0:T(8,128)S(1)} collective-permute-done((f32[2,216,128]{2,1,0:T(8,128)S(1)}, f32[2,216,128]{2,1,0:T(8,128)S(1)}, u32[]{:S(2)}, u32[]{:S(2)}) %collective-permute-start.20) | collective-permute-done | bytes 221216 | tf_op jit(solution)/shard_map/ppermute | solution.py:426
  64.4 3.8 %collective-permute-start.6 = (f32[2,216,128]{2,1,0:T(8,128)S(1)}, f32[2,216,128]{2,1,0:T(8,128)S(1)}, u32[]{:S(2)}, u32[]{:S(2)}) collective-permute-start(f32[2,216,128]{2,1,0:T(8,128)S(1)} %get-tuple-element.63), channel_id=1, source_target_pairs={{0,15},{1,10},{2,5},{3,0},{4,11},{5,14},{6,1},{7,4},{8,7},{9,2},{1... | collective-permute-start | bytes 663560 | tf_op jit(solution)/shard_map/ppermute | solution.py:426
  69.1 3.7 %shard_map.129 = (f32[2,216,128]{2,1,0:T(8,128)S(1)}, f32[2,216,128]{2,1,0:T(8,128)S(1)}, f32[2,216,128]{2,1,0:T(8,128)S(1)}, f32[2,216,128]{2,1,0:T(8,128)S(1)}...) custom-call(s32[6,16]{1,0:T(8,128)S(1)} %get-tuple-element.54.tab.ne, ...), custom_call_target="tpu_custom_call" | custom-call | flops 2000000000 | bytes 8000000 | tf_op jit(solution)/shard_map/pallas_call | solution.py:233
  72.9 1.9 %collective-permute-start.25 = (f32[1,216,128]{2,1,0:T(8,128)S(1)}, f32[1,216,128]{2,1,0:T(8,128)S(1)}, u32[]{:S(2)}, u32[]{:S(2)}) collective-permute-start(f32[1,216,128]{2,1,0:T(8,128)S(1)} %get-tuple-element.96), channel_id=1, source_target_pairs={{21,0},{16,1},{31,2},{26,3},{17,4},{20,5},{27,6},{30,7},{29,8},{24... | collective-permute-start | bytes 331784 | tf_op jit(solution)/shard_map/ppermute | solution.py:439
  75.2 1.7 %collective-permute-start.27 = (f32[1,216,128]{2,1,0:T(8,128)S(1)}, f32[1,216,128]{2,1,0:T(8,128)S(1)}, u32[]{:S(2)}, u32[]{:S(2)}) collective-permute-start(f32[1,216,128]{2,1,0:T(8,128)S(1)} %get-tuple-element.98), channel_id=1, source_target_pairs={{31,0},{26,1},{21,2},{16,3},{27,4},{30,5},{17,6},{20,7},{23,8},{18... | collective-permute-start | bytes 331784 | tf_op jit(solution)/shard_map/ppermute | solution.py:439
  76.9 3.6 %shard_map.127 = (f32[2,216,128]{2,1,0:T(8,128)S(1)}, f32[2,216,128]{2,1,0:T(8,128)S(1)}, f32[2,216,128]{2,1,0:T(8,128)S(1)}, f32[2,216,128]{2,1,0:T(8,128)S(1)}...) custom-call(s32[6,16]{1,0:T(8,128)S(1)} %get-tuple-element.54.tab.ne, ...), custom_call_target="tpu_custom_call" | custom-call | flops 2000000000 | bytes 8000000 | tf_op jit(solution)/shard_map/pallas_call | solution.py:233
  80.5 1.9 %collective-permute-start.7 = (f32[2,216,128]{2,1,0:T(8,128)S(1)}, f32[2,216,128]{2,1,0:T(8,128)S(1)}, u32[]{:S(2)}, u32[]{:S(2)}) collective-permute-start(f32[2,216,128]{2,1,0:T(8,128)S(1)} %get-tuple-element.72), channel_id=1, source_target_pairs={{0,1},{1,0},{2,3},{3,2},{4,5},{5,4},{6,7},{7,6},{8,9},{9,8},{10,11... | collective-permute-start | bytes 663560 | tf_op jit(solution)/shard_map/ppermute | solution.py:441
  82.4 4.4 %collective-permute-done.24.refs_4_ = f32[1,216,128]{2,1,0:T(8,128)S(1)} collective-permute-done((f32[1,216,128]{2,1,0:T(8,128)S(1)}, f32[1,216,128]{2,1,0:T(8,128)S(1)}, u32[]{:S(2)}, u32[]{:S(2)}) %collective-permute-start.24) | collective-permute-done | bytes 110624 | tf_op jit(solution)/shard_map/ppermute | solution.py:439
  86.8 1.8 %collective-permute-done.25.refs_5_ = f32[1,216,128]{2,1,0:T(8,128)S(1)} collective-permute-done((f32[1,216,128]{2,1,0:T(8,128)S(1)}, f32[1,216,128]{2,1,0:T(8,128)S(1)}, u32[]{:S(2)}, u32[]{:S(2)}) %collective-permute-start.25) | collective-permute-done | bytes 110624 | tf_op jit(solution)/shard_map/ppermute | solution.py:439
  89.3 3.2 %collective-permute-start.11 = (f32[2,216,128]{2,1,0:T(8,128)S(1)}, f32[2,216,128]{2,1,0:T(8,128)S(1)}, u32[]{:S(2)}, u32[]{:S(2)}) collective-permute-start(f32[2,216,128]{2,1,0:T(8,128)S(1)} %get-tuple-element.76), channel_id=1, source_target_pairs={{5,0},{0,1},{15,2},{10,3},{1,4},{4,5},{11,6},{14,7},{13,8},{8,9},{... | collective-permute-start | bytes 663560 | tf_op jit(solution)/shard_map/ppermute | solution.py:439
  93.1 4.7 %collective-permute-start.12 = (f32[2,216,128]{2,1,0:T(8,128)S(1)}, f32[2,216,128]{2,1,0:T(8,128)S(1)}, u32[]{:S(2)}, u32[]{:S(2)}) collective-permute-start(f32[2,216,128]{2,1,0:T(8,128)S(1)} %get-tuple-element.77), channel_id=1, source_target_pairs={{10,0},{15,1},{0,2},{5,3},{14,4},{11,5},{4,6},{1,7},{2,8},{7,9},{8... | collective-permute-start | bytes 663560 | tf_op jit(solution)/shard_map/ppermute | solution.py:439
  98.8 6.9 %collective-permute-done.9.refs_4_ = f32[2,216,128]{2,1,0:T(8,128)S(1)} collective-permute-done((f32[2,216,128]{2,1,0:T(8,128)S(1)}, f32[2,216,128]{2,1,0:T(8,128)S(1)}, u32[]{:S(2)}, u32[]{:S(2)}) %collective-permute-start.9) | collective-permute-done | bytes 221216 | tf_op jit(solution)/shard_map/ppermute | solution.py:441
  105.7 2.3 %collective-permute-start.22 = (f32[2,216,128]{2,1,0:T(8,128)S(1)}, f32[2,216,128]{2,1,0:T(8,128)S(1)}, u32[]{:S(2)}, u32[]{:S(2)}) collective-permute-start(f32[2,216,128]{2,1,0:T(8,128)S(1)} %get-tuple-element.93), channel_id=1, source_target_pairs={{0,2},{1,3},{2,0},{3,1},{4,6},{5,7},{6,4},{7,5},{8,10},{9,11},{10,... | collective-permute-start | bytes 663560 | tf_op jit(solution)/shard_map/ppermute | solution.py:441
  108.0 4.3 %collective-permute-done.12.refs_7_ = f32[2,216,128]{2,1,0:T(8,128)S(1)} collective-permute-done((f32[2,216,128]{2,1,0:T(8,128)S(1)}, f32[2,216,128]{2,1,0:T(8,128)S(1)}, u32[]{:S(2)}, u32[]{:S(2)}) %collective-permute-start.12) | collective-permute-done | bytes 221216 | tf_op jit(solution)/shard_map/ppermute | solution.py:439
  112.3 2.1 %collective-permute-done.13.refs_8_ = f32[2,216,128]{2,1,0:T(8,128)S(1)} collective-permute-done((f32[2,216,128]{2,1,0:T(8,128)S(1)}, f32[2,216,128]{2,1,0:T(8,128)S(1)}, u32[]{:S(2)}, u32[]{:S(2)}) %collective-permute-start.13) | collective-permute-done | bytes 221216 | tf_op jit(solution)/shard_map/ppermute | solution.py:439
  115.5 3.6 %collective-permute-start.30 = (f32[1,216,128]{2,1,0:T(8,128)S(1)}, f32[1,216,128]{2,1,0:T(8,128)S(1)}, u32[]{:S(2)}, u32[]{:S(2)}) collective-permute-start(f32[1,216,128]{2,1,0:T(8,128)S(1)} %get-tuple-element.101), channel_id=1, source_target_pairs={{26,0},{31,1},{16,2},{21,3},{30,4},{27,5},{20,6},{17,7},{18,8},{23... | collective-permute-start | bytes 331784 | tf_op jit(solution)/shard_map/ppermute | solution.py:439
  119.1 1.3 collective-permute-done.22.refs_2_
  121.5 8.3 %collective-permute-done.23.refs_3_ = f32[2,216,128]{2,1,0:T(8,128)S(1)} collective-permute-done((f32[2,216,128]{2,1,0:T(8,128)S(1)}, f32[2,216,128]{2,1,0:T(8,128)S(1)}, u32[]{:S(2)}, u32[]{:S(2)}) %collective-permute-start.23) | collective-permute-done | bytes 221216 | tf_op jit(solution)/shard_map/ppermute | solution.py:441
  130.8 1.6 %shard_map.132 = f32[1728,128]{1,0:T(8,128)} custom-call(s32[6,16]{1,0:T(8,128)S(1)} %get-tuple-element.54.tab.near_tab, s32[2,16]{1,0:T(2,128)S(1)} %get-tuple-element.55.far_tab, f32[1728,128]{1,0:T(8,128)S(1)} %shard_map.131.base, f32[1,216,128]{2,1,0:T(8,128)S(1)} %collective-permute-done.28.refs_0_, f32[1,216,128]{2,1,0:T(8,128)S(1)} %collective-permute-done.29.refs_1_, ...), custom_call_target="tpu_custom_call" | custom-call | tf_op jit(solution)/shard_map/pallas_call | solution.py:452
  (63 shorter events, 13.5 us)
Async XLA Ops:
  4.8 19.9 %collective-permute-start = (f32[2,216,128]{2,1,0:T(8,128)}, f32[2,216,128]{2,1,0:T(8,128)S(1)}, u32[]{:S(2)}, u32[]{:S(2)}) collective-permute-start(f32[2,216,128]{2,1,0:T(8,128)} %get-tuple-element.57), channel_id=1, source_target_pairs={{0,1},{1,0},{2,3},{3,2},{4,5},{5,4},{6,7},{7,6},{8,9},{9,8},{10,11... | collective-permute-start | bytes 663560 | tf_op jit(solution)/shard_map/ppermute | solution.py:405
  5.4 19.9 %collective-permute-start.1 = (f32[2,216,128]{2,1,0:T(8,128)}, f32[2,216,128]{2,1,0:T(8,128)S(1)}, u32[]{:S(2)}, u32[]{:S(2)}) collective-permute-start(f32[2,216,128]{2,1,0:T(8,128)} %get-tuple-element.58), channel_id=1, source_target_pairs={{0,2},{1,3},{2,0},{3,1},{4,6},{5,7},{6,4},{7,5},{8,10},{9,11},{10,... | collective-permute-start | bytes 663560 | tf_op jit(solution)/shard_map/ppermute | solution.py:405
  8.0 18.6 %collective-permute-start.14 = (f32[2,216,128]{2,1,0:T(8,128)S(1)}, f32[2,216,128]{2,1,0:T(8,128)S(1)}, u32[]{:S(2)}, u32[]{:S(2)}) collective-permute-start(f32[2,216,128]{2,1,0:T(8,128)S(1)} %get-tuple-element.80), channel_id=1, source_target_pairs={{0,1},{1,0},{2,3},{3,2},{4,5},{5,4},{6,7},{7,6},{8,9},{9,8},{10,11... | collective-permute-start | bytes 663560 | tf_op jit(solution)/shard_map/ppermute | solution.py:405
  8.1 21.5 %collective-permute-start.15 = (f32[2,216,128]{2,1,0:T(8,128)S(1)}, f32[2,216,128]{2,1,0:T(8,128)S(1)}, u32[]{:S(2)}, u32[]{:S(2)}) collective-permute-start(f32[2,216,128]{2,1,0:T(8,128)S(1)} %get-tuple-element.81), channel_id=1, source_target_pairs={{0,2},{1,3},{2,0},{3,1},{4,6},{5,7},{6,4},{7,5},{8,10},{9,11},{10,... | collective-permute-start | bytes 663560 | tf_op jit(solution)/shard_map/ppermute | solution.py:405
  9.8 12.5 %all-to-all-start = ((s32[8,1,18]{2,1,0:T(1,128)}), s32[8,1,18]{2,1,0:T(1,128)S(1)}, u32[]{:S(2)}, u32[]{:S(2)}) async-start(s32[8,1,18]{2,1,0:T(1,128)} %broadcast_select_fusion), calls=%async_computation | async-start | bytes 8192 | tf_op jit(solution)/shard_map/all_to_all | solution.py:383
  15.8 16.0 %collective-permute-start.16 = (f32[2,216,128]{2,1,0:T(8,128)S(1)}, f32[2,216,128]{2,1,0:T(8,128)S(1)}, u32[]{:S(2)}, u32[]{:S(2)}) collective-permute-start(f32[2,216,128]{2,1,0:T(8,128)S(1)} %get-tuple-element.82), channel_id=1, source_target_pairs={{0,3},{1,2},{2,1},{3,0},{4,7},{5,6},{6,5},{7,4},{8,11},{9,10},{10,... | collective-permute-start | bytes 663560 | tf_op jit(solution)/shard_map/ppermute | solution.py:405
  24.7 26.7 %collective-permute-start.17 = (f32[2,216,128]{2,1,0:T(8,128)S(1)}, f32[2,216,128]{2,1,0:T(8,128)S(1)}, u32[]{:S(2)}, u32[]{:S(2)}) collective-permute-start(f32[2,216,128]{2,1,0:T(8,128)S(1)} %get-tuple-element.83), channel_id=1, source_target_pairs={{0,16},{1,21},{2,26},{3,31},{4,20},{5,17},{6,30},{7,27},{8,24},{9,... | collective-permute-start | bytes 663560 | tf_op jit(solution)/shard_map/ppermute | solution.py:426
  25.3 30.1 %collective-permute-start.18 = (f32[2,216,128]{2,1,0:T(8,128)S(1)}, f32[2,216,128]{2,1,0:T(8,128)S(1)}, u32[]{:S(2)}, u32[]{:S(2)}) collective-permute-start(f32[2,216,128]{2,1,0:T(8,128)S(1)} %get-tuple-element.84), channel_id=1, source_target_pairs={{0,21},{1,16},{2,31},{3,26},{4,17},{5,20},{6,27},{7,30},{8,29},{9,... | collective-permute-start | bytes 663560 | tf_op jit(solution)/shard_map/ppermute | solution.py:426
  26.6 35.8 %collective-permute-start.19 = (f32[2,216,128]{2,1,0:T(8,128)S(1)}, f32[2,216,128]{2,1,0:T(8,128)S(1)}, u32[]{:S(2)}, u32[]{:S(2)}) collective-permute-start(f32[2,216,128]{2,1,0:T(8,128)S(1)} %get-tuple-element.85), channel_id=1, source_target_pairs={{0,26},{1,31},{2,16},{3,21},{4,30},{5,27},{6,20},{7,17},{8,18},{9,... | collective-permute-start | bytes 663560 | tf_op jit(solution)/shard_map/ppermute | solution.py:426
  29.6 34.7 %collective-permute-start.20 = (f32[2,216,128]{2,1,0:T(8,128)S(1)}, f32[2,216,128]{2,1,0:T(8,128)S(1)}, u32[]{:S(2)}, u32[]{:S(2)}) collective-permute-start(f32[2,216,128]{2,1,0:T(8,128)S(1)} %get-tuple-element.86), channel_id=1, source_target_pairs={{0,31},{1,26},{2,21},{3,16},{4,27},{5,30},{6,17},{7,20},{8,23},{9,... | collective-permute-start | bytes 663560 | tf_op jit(solution)/shard_map/ppermute | solution.py:426
  31.7 41.0 %collective-permute-start.2 = (f32[2,216,128]{2,1,0:T(8,128)S(1)}, f32[2,216,128]{2,1,0:T(8,128)S(1)}, u32[]{:S(2)}, u32[]{:S(2)}) collective-permute-start(f32[2,216,128]{2,1,0:T(8,128)S(1)} %get-tuple-element.59), channel_id=1, source_target_pairs={{0,3},{1,2},{2,1},{3,0},{4,7},{5,6},{6,5},{7,4},{8,11},{9,10},{10,... | collective-permute-start | bytes 663560 | tf_op jit(solution)/shard_map/ppermute | solution.py:405
  51.4 21.4 %collective-permute-start.3 = (f32[2,216,128]{2,1,0:T(8,128)S(1)}, f32[2,216,128]{2,1,0:T(8,128)S(1)}, u32[]{:S(2)}, u32[]{:S(2)}) collective-permute-start(f32[2,216,128]{2,1,0:T(8,128)S(1)} %get-tuple-element.60), channel_id=1, source_target_pairs={{0,0},{1,5},{2,10},{3,15},{4,4},{5,1},{6,14},{7,11},{8,8},{9,13},{... | collective-permute-start | bytes 663560 | tf_op jit(solution)/shard_map/ppermute | solution.py:426
  55.4 19.4 %collective-permute-start.4 = (f32[2,216,128]{2,1,0:T(8,128)S(1)}, f32[2,216,128]{2,1,0:T(8,128)S(1)}, u32[]{:S(2)}, u32[]{:S(2)}) collective-permute-start(f32[2,216,128]{2,1,0:T(8,128)S(1)} %get-tuple-element.61), channel_id=1, source_target_pairs={{0,5},{1,0},{2,15},{3,10},{4,1},{5,4},{6,11},{7,14},{8,13},{9,8},{... | collective-permute-start | bytes 663560 | tf_op jit(solution)/shard_map/ppermute | solution.py:426
  62.4 12.8 %collective-permute-start.5 = (f32[2,216,128]{2,1,0:T(8,128)S(1)}, f32[2,216,128]{2,1,0:T(8,128)S(1)}, u32[]{:S(2)}, u32[]{:S(2)}) collective-permute-start(f32[2,216,128]{2,1,0:T(8,128)S(1)} %get-tuple-element.62), channel_id=1, source_target_pairs={{0,10},{1,15},{2,0},{3,5},{4,14},{5,11},{6,4},{7,1},{8,2},{9,7},{1... | collective-permute-start | bytes 663560 | tf_op jit(solution)/shard_map/ppermute | solution.py:426
  64.4 12.5 %collective-permute-start.6 = (f32[2,216,128]{2,1,0:T(8,128)S(1)}, f32[2,216,128]{2,1,0:T(8,128)S(1)}, u32[]{:S(2)}, u32[]{:S(2)}) collective-permute-start(f32[2,216,128]{2,1,0:T(8,128)S(1)} %get-tuple-element.63), channel_id=1, source_target_pairs={{0,15},{1,10},{2,5},{3,0},{4,11},{5,14},{6,1},{7,4},{8,7},{9,2},{1... | collective-permute-start | bytes 663560 | tf_op jit(solution)/shard_map/ppermute | solution.py:426
  72.8 14.0 %collective-permute-start.24 = (f32[1,216,128]{2,1,0:T(8,128)S(1)}, f32[1,216,128]{2,1,0:T(8,128)S(1)}, u32[]{:S(2)}, u32[]{:S(2)}) collective-permute-start(f32[1,216,128]{2,1,0:T(8,128)S(1)} %get-tuple-element.95), channel_id=1, source_target_pairs={{16,0},{21,1},{26,2},{31,3},{20,4},{17,5},{30,6},{27,7},{24,8},{29... | collective-permute-start | bytes 331784 | tf_op jit(solution)/shard_map/ppermute | solution.py:439
  72.9 15.7 %collective-permute-start.25 = (f32[1,216,128]{2,1,0:T(8,128)S(1)}, f32[1,216,128]{2,1,0:T(8,128)S(1)}, u32[]{:S(2)}, u32[]{:S(2)}) collective-permute-start(f32[1,216,128]{2,1,0:T(8,128)S(1)} %get-tuple-element.96), channel_id=1, source_target_pairs={{21,0},{16,1},{31,2},{26,3},{17,4},{20,5},{27,6},{30,7},{29,8},{24... | collective-permute-start | bytes 331784 | tf_op jit(solution)/shard_map/ppermute | solution.py:439
  74.8 13.8 %collective-permute-start.26 = (f32[1,216,128]{2,1,0:T(8,128)S(1)}, f32[1,216,128]{2,1,0:T(8,128)S(1)}, u32[]{:S(2)}, u32[]{:S(2)}) collective-permute-start(f32[1,216,128]{2,1,0:T(8,128)S(1)} %get-tuple-element.97), channel_id=1, source_target_pairs={{26,0},{31,1},{16,2},{21,3},{30,4},{27,5},{20,6},{17,7},{18,8},{23... | collective-permute-start | bytes 331784 | tf_op jit(solution)/shard_map/ppermute | solution.py:439
  75.2 14.1 %collective-permute-start.27 = (f32[1,216,128]{2,1,0:T(8,128)S(1)}, f32[1,216,128]{2,1,0:T(8,128)S(1)}, u32[]{:S(2)}, u32[]{:S(2)}) collective-permute-start(f32[1,216,128]{2,1,0:T(8,128)S(1)} %get-tuple-element.98), channel_id=1, source_target_pairs={{31,0},{26,1},{21,2},{16,3},{27,4},{30,5},{17,6},{20,7},{23,8},{18... | collective-permute-start | bytes 331784 | tf_op jit(solution)/shard_map/ppermute | solution.py:439
  80.5 12.5 %collective-permute-start.7 = (f32[2,216,128]{2,1,0:T(8,128)S(1)}, f32[2,216,128]{2,1,0:T(8,128)S(1)}, u32[]{:S(2)}, u32[]{:S(2)}) collective-permute-start(f32[2,216,128]{2,1,0:T(8,128)S(1)} %get-tuple-element.72), channel_id=1, source_target_pairs={{0,1},{1,0},{2,3},{3,2},{4,5},{5,4},{6,7},{7,6},{8,9},{9,8},{10,11... | collective-permute-start | bytes 663560 | tf_op jit(solution)/shard_map/ppermute | solution.py:441
  86.8 11.0 %collective-permute-start.8 = (f32[2,216,128]{2,1,0:T(8,128)S(1)}, f32[2,216,128]{2,1,0:T(8,128)S(1)}, u32[]{:S(2)}, u32[]{:S(2)}) collective-permute-start(f32[2,216,128]{2,1,0:T(8,128)S(1)} %get-tuple-element.73), channel_id=1, source_target_pairs={{0,2},{1,3},{2,0},{3,1},{4,6},{5,7},{6,4},{7,5},{8,10},{9,11},{10,... | collective-permute-start | bytes 663560 | tf_op jit(solution)/shard_map/ppermute | solution.py:441
  88.6 17.1 %collective-permute-start.9 = (f32[2,216,128]{2,1,0:T(8,128)S(1)}, f32[2,216,128]{2,1,0:T(8,128)S(1)}, u32[]{:S(2)}, u32[]{:S(2)}) collective-permute-start(f32[2,216,128]{2,1,0:T(8,128)S(1)} %get-tuple-element.74), channel_id=1, source_target_pairs={{0,3},{1,2},{2,1},{3,0},{4,7},{5,6},{6,5},{7,4},{8,11},{9,10},{10,... | collective-permute-start | bytes 663560 | tf_op jit(solution)/shard_map/ppermute | solution.py:441
  88.6 17.1 %collective-permute-start.10 = (f32[2,216,128]{2,1,0:T(8,128)S(1)}, f32[2,216,128]{2,1,0:T(8,128)S(1)}, u32[]{:S(2)}, u32[]{:S(2)}) collective-permute-start(f32[2,216,128]{2,1,0:T(8,128)S(1)} %get-tuple-element.75), channel_id=1, source_target_pairs={{0,0},{5,1},{10,2},{15,3},{4,4},{1,5},{14,6},{11,7},{8,8},{13,9},{... | collective-permute-start | bytes 663560 | tf_op jit(solution)/shard_map/ppermute | solution.py:439
  89.3 18.7 %collective-permute-start.11 = (f32[2,216,128]{2,1,0:T(8,128)S(1)}, f32[2,216,128]{2,1,0:T(8,128)S(1)}, u32[]{:S(2)}, u32[]{:S(2)}) collective-permute-start(f32[2,216,128]{2,1,0:T(8,128)S(1)} %get-tuple-element.76), channel_id=1, source_target_pairs={{5,0},{0,1},{15,2},{10,3},{1,4},{4,5},{11,6},{14,7},{13,8},{8,9},{... | collective-permute-start | bytes 663560 | tf_op jit(solution)/shard_map/ppermute | solution.py:439
  93.1 19.2 %collective-permute-start.12 = (f32[2,216,128]{2,1,0:T(8,128)S(1)}, f32[2,216,128]{2,1,0:T(8,128)S(1)}, u32[]{:S(2)}, u32[]{:S(2)}) collective-permute-start(f32[2,216,128]{2,1,0:T(8,128)S(1)} %get-tuple-element.77), channel_id=1, source_target_pairs={{10,0},{15,1},{0,2},{5,3},{14,4},{11,5},{4,6},{1,7},{2,8},{7,9},{8... | collective-permute-start | bytes 663560 | tf_op jit(solution)/shard_map/ppermute | solution.py:439
  97.8 16.6 %collective-permute-start.13 = (f32[2,216,128]{2,1,0:T(8,128)S(1)}, f32[2,216,128]{2,1,0:T(8,128)S(1)}, u32[]{:S(2)}, u32[]{:S(2)}) collective-permute-start(f32[2,216,128]{2,1,0:T(8,128)S(1)} %get-tuple-element.78), channel_id=1, source_target_pairs={{15,0},{10,1},{5,2},{0,3},{11,4},{14,5},{1,6},{4,7},{7,8},{2,9},{1... | collective-permute-start | bytes 663560 | tf_op jit(solution)/shard_map/ppermute | solution.py:439
  105.7 14.7 %collective-permute-start.22 = (f32[2,216,128]{2,1,0:T(8,128)S(1)}, f32[2,216,128]{2,1,0:T(8,128)S(1)}, u32[]{:S(2)}, u32[]{:S(2)}) collective-permute-start(f32[2,216,128]{2,1,0:T(8,128)S(1)} %get-tuple-element.93), channel_id=1, source_target_pairs={{0,2},{1,3},{2,0},{3,1},{4,6},{5,7},{6,4},{7,5},{8,10},{9,11},{10,... | collective-permute-start | bytes 663560 | tf_op jit(solution)/shard_map/ppermute | solution.py:441
  108.0 21.8 %collective-permute-start.23 = (f32[2,216,128]{2,1,0:T(8,128)S(1)}, f32[2,216,128]{2,1,0:T(8,128)S(1)}, u32[]{:S(2)}, u32[]{:S(2)}) collective-permute-start(f32[2,216,128]{2,1,0:T(8,128)S(1)} %get-tuple-element.94), channel_id=1, source_target_pairs={{0,3},{1,2},{2,1},{3,0},{4,7},{5,6},{6,5},{7,4},{8,11},{9,10},{10,... | collective-permute-start | bytes 663560 | tf_op jit(solution)/shard_map/ppermute | solution.py:441
  112.3 18.5 %collective-permute-start.28 = (f32[1,216,128]{2,1,0:T(8,128)S(1)}, f32[1,216,128]{2,1,0:T(8,128)S(1)}, u32[]{:S(2)}, u32[]{:S(2)}) collective-permute-start(f32[1,216,128]{2,1,0:T(8,128)S(1)} %get-tuple-element.99), channel_id=1, source_target_pairs={{16,0},{21,1},{26,2},{31,3},{20,4},{17,5},{30,6},{27,7},{24,8},{29... | collective-permute-start | bytes 331784 | tf_op jit(solution)/shard_map/ppermute | solution.py:439
  114.3 16.4 %collective-permute-start.29 = (f32[1,216,128]{2,1,0:T(8,128)S(1)}, f32[1,216,128]{2,1,0:T(8,128)S(1)}, u32[]{:S(2)}, u32[]{:S(2)}) collective-permute-start(f32[1,216,128]{2,1,0:T(8,128)S(1)} %get-tuple-element.100), channel_id=1, source_target_pairs={{21,0},{16,1},{31,2},{26,3},{17,4},{20,5},{27,6},{30,7},{29,8},{24... | collective-permute-start | bytes 331784 | tf_op jit(solution)/shard_map/ppermute | solution.py:439
  115.5 15.3 %collective-permute-start.30 = (f32[1,216,128]{2,1,0:T(8,128)S(1)}, f32[1,216,128]{2,1,0:T(8,128)S(1)}, u32[]{:S(2)}, u32[]{:S(2)}) collective-permute-start(f32[1,216,128]{2,1,0:T(8,128)S(1)} %get-tuple-element.101), channel_id=1, source_target_pairs={{26,0},{31,1},{16,2},{21,3},{30,4},{27,5},{20,6},{17,7},{18,8},{23... | collective-permute-start | bytes 331784 | tf_op jit(solution)/shard_map/ppermute | solution.py:439
  120.4 10.4 %collective-permute-start.31 = (f32[1,216,128]{2,1,0:T(8,128)S(1)}, f32[1,216,128]{2,1,0:T(8,128)S(1)}, u32[]{:S(2)}, u32[]{:S(2)}) collective-permute-start(f32[1,216,128]{2,1,0:T(8,128)S(1)} %get-tuple-element.102), channel_id=1, source_target_pairs={{31,0},{26,1},{21,2},{16,3},{27,4},{30,5},{17,6},{20,7},{23,8},{18... | collective-permute-start | bytes 331784 | tf_op jit(solution)/shard_map/ppermute | solution.py:439
  (8 other events, 326.0 us)
